TPU v7x, 128 devices: a whole 4x4x4 slice. The times are simulated.
128 devices in a mesh: section: 2 (over core), expert: 64 (over x, z, y).
Axes of the slice: x: 4, y: 4, z: 4, core: 2. Of those that a mesh axis runs over, the one named last changes fastest.
Arguments:
- grad_out: bfloat16 [2, 8192, 4096], P('section', 'expert'), may hold values from -6 to 6
- saved_hidden: bfloat16 [2, 8192, 8, 1024], P('section', 'expert'), may hold values from -6 to 6
- routes: int32 [2, 8192, 8], P('section', 'expert'), may hold values from 0 to 63, all different within a row; in each aligned block of 128 rows (0 to 127, 128 to 255, ..., all dimensions but the last counted through in order) at most 24 rows name the same one
- scores: float32 [2, 8192, 8], P('section', 'expert'), may hold values from 0.02 to 0.98
- down_weight: bfloat16 [2, 64, 1024, 4096], P('section', 'expert'), may hold values from -0.1875 to 0.1875
- router: bfloat16 [2, 64, 4096], P('section'), may hold values from -0.59765625 to 0.59765625
Outputs:
- weight_grad: bfloat16 [2, 64, 1024, 4096], P('section', 'expert')
- handed: bfloat16 [2, 8192, 4096], P('section', 'expert')
Inputs may be any that keep to these rules, and one draw needn't show every extreme that they name: `routes`: each token names 8 different experts. Among the 128 tokens of one index of expert (aligned blocks), no expert is named more than 24 times, and in every draw some expert is named exactly 24 times in some block.
All inputs are finite; a program needn't handle non-finite values.
Results may differ from a plain program's by a relative error of at most 0.007.
Values may be sent and summed in bfloat16 or wider, within the bound.
A program may use at most 128 MiB of HBM per device.

v0:
```python
import jax
import jax.numpy as jnp
from jax import lax
from jax.sharding import PartitionSpec as P


def passed_along(array, axis, by):
    size = lax.axis_size(axis)
    return lax.ppermute(array, axis, [(i, (i + by) % size) for i in range(size)])


def slot_layout(route_ids, n_experts, capacity):
    flat_routes = route_ids.reshape(-1)
    entries = flat_routes.shape[0]
    onehot = (flat_routes[:, None] == jnp.arange(n_experts, dtype=jnp.int32)[None, :]).astype(
        jnp.int32
    )
    running = jnp.cumsum(onehot, axis=0)
    slot_index = jnp.sum(running * onehot, axis=1) - 1
    target = flat_routes * capacity + slot_index
    source = jnp.full((n_experts * capacity,), entries, jnp.int32)
    source = source.at[target].set(jnp.arange(entries, dtype=jnp.int32))
    return (target, source)


def expert_derivs(grad_in, hidden_in, expert_down):
    projected = lax.dot_general(
        grad_in, expert_down, (((1,), (1,)), ((), ())), preferred_element_type=jnp.float32
    )
    return jnp.sum(projected * hidden_in.astype(jnp.float32), axis=1)


def weight_pass(grad_in, hidden_in, weight_in):
    scaled = (weight_in.astype(jnp.float32)[:, None] * grad_in.astype(jnp.float32)).astype(
        jnp.bfloat16
    )
    weight_grads = lax.dot_general(
        hidden_in, scaled, (((0,), (0,)), ((), ())), preferred_element_type=jnp.float32
    )
    return weight_grads.astype(jnp.bfloat16)


def body(grad_out, saved_hidden, routes, scores, down_weight, router):
    grad_rows = grad_out[0]
    hidden_rows = saved_hidden[0]
    route_ids = routes[0]
    score_rows = scores[0]
    expert_down = down_weight[0, 0]
    router_rows = router[0]
    n_tokens, n_routes, hidden_width = hidden_rows.shape
    model_width = grad_rows.shape[1]
    n_experts = router_rows.shape[0]
    capacity = 3 * n_tokens * n_routes // (2 * n_experts)
    entries = n_tokens * n_routes
    target, source = slot_layout(route_ids, n_experts, capacity)
    filled = source < entries
    safe_index = jnp.minimum(source, entries - 1)
    score_total = jnp.sum(score_rows, axis=1, keepdims=True)
    weights = score_rows / score_total
    weights_low = weights.astype(jnp.bfloat16).reshape(-1)
    grad_slots = jnp.where(
        filled[:, None], grad_rows[safe_index // n_routes], jnp.zeros((), jnp.bfloat16)
    )
    grad_slots = grad_slots.reshape(n_experts, capacity, model_width)
    hidden_slots = jnp.where(
        filled[:, None],
        hidden_rows.reshape(entries, hidden_width)[safe_index],
        jnp.zeros((), jnp.bfloat16),
    )
    hidden_slots = hidden_slots.reshape(n_experts, capacity, hidden_width)
    weight_slots = jnp.where(filled, weights_low[safe_index], jnp.zeros((), jnp.bfloat16)).reshape(
        n_experts, capacity
    )
    grad_recv, hidden_recv, weight_recv = (
        lax.all_to_all(grad_slots, "expert", split_axis=0, concat_axis=0, tiled=True),
        lax.all_to_all(hidden_slots, "expert", split_axis=0, concat_axis=0, tiled=True),
        lax.all_to_all(weight_slots, "expert", split_axis=0, concat_axis=0, tiled=True),
    )
    n_source = grad_recv.shape[0]
    derivs = expert_derivs(
        grad_recv.reshape(-1, model_width), hidden_recv.reshape(-1, hidden_width), expert_down
    )
    returned = lax.all_to_all(
        derivs.reshape(n_source, capacity), "expert", split_axis=0, concat_axis=0, tiled=True
    )
    weight_out = weight_pass(
        grad_recv.reshape(-1, model_width),
        hidden_recv.reshape(-1, hidden_width),
        weight_recv.reshape(-1),
    )
    derivs_home = returned.reshape(-1)[target].reshape(n_tokens, n_routes)
    center = jnp.sum(weights * derivs_home, axis=1, keepdims=True)
    logit_grad = score_rows * (1.0 - score_rows) / score_total * (derivs_home - center)
    expert_ids = jnp.arange(n_experts, dtype=jnp.int32)
    dense_grad = jnp.sum(
        jnp.where(route_ids[:, :, None] == expert_ids[None, None, :], logit_grad[:, :, None], 0.0),
        axis=1,
    )
    input_grad = grad_rows.astype(jnp.float32) + jnp.dot(
        dense_grad, router_rows.astype(jnp.float32)
    )
    handed = passed_along(input_grad.astype(jnp.bfloat16), "section", -1)
    return (weight_out[None, None], handed[None])


def solution(mesh):
    return jax.shard_map(
        body,
        mesh=mesh,
        in_specs=(
            P("section", "expert", None),
            P("section", "expert", None, None),
            P("section", "expert", None),
            P("section", "expert", None),
            P("section", "expert", None, None),
            P("section", None, None),
        ),
        out_specs=(P("section", "expert", None, None), P("section", "expert", None)),
        check_vma=False,
    )
```

profile of v0, /device:TPU:1, one launch (start us, length us, event | category | flops | bytes accessed | tf_op | source)
XLA Modules:
  0.0 385.7 jit_solution(10502944268737782340)
XLA Ops:
  0.6 0.8 broadcast_multiply_fusion
  1.5 0.8 copy.49
  2.7 18.0 %reduce-window.6 = s32[64,8,128]{2,1,0:T(8,128)S(1)} reduce-window(s32[64,8,128]{2,1,0:T(8,128)S(1)} %fusion.11, s32[]{:T(128)} %constant.15.clone.1), window={size=1x1x128 pad=0_0x0_0x127_0}, to_apply=%region_0.0 | reduce-window | flops 8323072 | bytes 524292 | tf_op jit(solution)/shard_map/reduce-window
  21.4 4.3 %scatter_custom_fusion = s32[1536]{0:T(1024)S(1)} fusion(s32[1024]{0:T(1024)S(1)} %bitcast.62, s32[1024]{0:T(1024)S(1)} %iota.15, s32[]{:T(128)} %constant.13.clone.1), kind=kCustom, calls=%fused_computation.47 | custom fusion | bytes 6148 | tf_op jit(solution)/shard_map/scatter | solution.py:22
  25.7 0.8 copy.53
  27.5 5.8 %gather_fusion = bf16[1536,1024]{1,0:T(8,128)(2,1)} fusion(bf16[1024,1024]{1,0:T(8,128)(2,1)S(1)} %bitcast.53, s32[2048]{0:T(1024)S(1)} %get-tuple-element.7), kind=kCustom, calls=%fused_computation | custom fusion | bytes 6297600 | tf_op jit(solution)/shard_map/gather | solution.py:67
  33.3 9.5 %gather_fusion.1 = bf16[1536]{0:T(1024)(128)(2,1)S(1)} fusion(bf16[1024]{0:T(1024)(128)(2,1)S(1)} %divide_convert_fusion, s32[2048]{0:T(1024)S(1)} %get-tuple-element.7), kind=kCustom, calls=%fused_computation.1 | custom fusion | bytes 12288 | tf_op jit(solution)/shard_map/gather | solution.py:71
  42.9 3.3 broadcast_select_fusion.1
  46.1 12.2 %all-to-all-start = ((bf16[64,24,1024]{2,1,0:T(8,128)(2,1)}), bf16[64,24,1024]{2,1,0:T(8,128)(2,1)}, u32[]{:S(2)}, u32[]{:S(2)}) async-start(bf16[64,24,1024]{2,1,0:T(8,128)(2,1)} %broadcast_select_fusion.1), calls=%async_computation | async-start | bytes 6291456 | tf_op jit(solution)/shard_map/all_to_all | solution.py:76
  58.3 9.5 %gather_fusion.2 = bf16[1536,4096]{1,0:T(8,128)(2,1)} fusion(bf16[128,4096]{1,0:T(8,128)(2,1)S(1)} %bitcast.54, s32[2048]{0:T(1024)S(1)} %get-tuple-element.6), kind=kCustom, calls=%fused_computation.2 | custom fusion | bytes 25171968 | tf_op jit(solution)/shard_map/gather | solution.py:62
  67.9 10.7 %broadcast_select_fusion = bf16[64,24,4096]{2,1,0:T(8,128)(2,1)} fusion(bf16[64,24,4096]{2,1,0:T(8,128)(2,1)} %bitcast.55, pred[64,24]{1,0:T(8,128)(4,1)S(1)} %broadcast_in_dim.65), kind=kLoop, calls=%fused_computation.9 | loop fusion | flops 6291456 | bytes 25167360 | tf_op jit(solution)/shard_map/jit(_where)/select_n | solution.py:61
  78.6 19.8 %all-to-all-done = bf16[64,24,1024]{2,1,0:T(8,128)(2,1)} async-done(((bf16[64,24,1024]{2,1,0:T(8,128)(2,1)}), bf16[64,24,1024]{2,1,0:T(8,128)(2,1)}, u32[]{:S(2)}, u32[]{:S(2)}) %all-to-all-start) | async-done | bytes 3145760 | tf_op jit(solution)/shard_map/all_to_all | solution.py:76
  98.4 12.8 %all-to-all-start.2 = ((bf16[64,24,4096]{2,1,0:T(8,128)(2,1)}), bf16[64,24,4096]{2,1,0:T(8,128)(2,1)}, u32[]{:S(2)}, u32[]{:S(2)}) async-start(bf16[64,24,4096]{2,1,0:T(8,128)(2,1)} %broadcast_select_fusion), calls=%async_computation.2 | async-start | bytes 25165824 | tf_op jit(solution)/shard_map/all_to_all | solution.py:75
  111.9 5.3 %bitcast_convert_fusion.1 = f32[1536,1024]{1,0:T(8,128)} fusion(bf16[64,24,1024]{2,1,0:T(8,128)(2,1)} %all-to-all-done), kind=kLoop, calls=%fused_computation.16 | loop fusion | flops 1572864 | bytes 9437184 | tf_op jit(solution)/shard_map/convert_element_type | solution.py:30
  117.2 6.7 %copy.56 = f32[1536,1024]{0,1:T(8,128)} copy(f32[1536,1024]{1,0:T(8,128)} %bitcast_convert_fusion.1) | data formatting | bytes 12582912 | tf_op jit(solution)/shard_map/convert_element_type | solution.py:30
  123.9 169.1 %all-to-all-done.2 = bf16[64,24,4096]{2,1,0:T(8,128)(2,1)} async-done(((bf16[64,24,4096]{2,1,0:T(8,128)(2,1)}), bf16[64,24,4096]{2,1,0:T(8,128)(2,1)}, u32[]{:S(2)}, u32[]{:S(2)}) %all-to-all-start.2) | async-done | bytes 12582944 | tf_op jit(solution)/shard_map/all_to_all | solution.py:75
  292.9 21.3 %all-to-all-start.1 = ((bf16[64,1,24]{2,1,0:T(2,128)(2,1)}), bf16[64,1,24]{2,1,0:T(2,128)(2,1)S(1)}, u32[]{:S(2)}, u32[]{:S(2)}) async-start(bf16[64,1,24]{2,1,0:T(2,128)(2,1)} %all_to_all.24), calls=%async_computation.1 | async-start | bytes 65536 | tf_op jit(solution)/shard_map/all_to_all | solution.py:77
  314.3 19.0 %multiply_reduce_fusion = f32[1536]{0:T(1024)S(1)} fusion(f32[1536,1024]{0,1:T(8,128)} %copy.56, bf16[1536,4096]{1,0:T(8,128)(2,1)} %bitcast.13, bf16[1,1,1024,4096]{3,2,1,0:T(8,128)(2,1)} %param.10), kind=kOutput, calls=%fused_computation.13 | convolution fusion | flops 12888045568 | bytes 27269120 | tf_op jit(solution)/shard_map/dot_general | solution.py:27
  334.0 9.6 %all-to-all-start.3 = ((f32[64,1,24]{2,1,0:T(1,128)}), f32[64,1,24]{2,1,0:T(1,128)S(1)}, u32[]{:S(2)}, u32[]{:S(2)}) async-start(f32[64,1,24]{2,1,0:T(1,128)} %bitcast.16), calls=%async_computation.3 | async-start | bytes 65536 | tf_op jit(solution)/shard_map/all_to_all | solution.py:83
  343.6 8.3 %all-to-all-done.3 = f32[64,1,24]{2,1,0:T(1,128)S(1)} async-done(((f32[64,1,24]{2,1,0:T(1,128)}), f32[64,1,24]{2,1,0:T(1,128)S(1)}, u32[]{:S(2)}, u32[]{:S(2)}) %all-to-all-start.3) | async-done | bytes 6176 | tf_op jit(solution)/shard_map/all_to_all | solution.py:83
  353.3 6.2 %gather_fusion.3 = f32[1024]{0:T(1024)S(1)} fusion(f32[1536]{0:T(1024)S(1)} %reshape.157, s32[1024]{0:T(1024)S(1)} %broadcast_clamp_fusion), kind=kCustom, calls=%fused_computation.3 | custom fusion | bytes 12288 | tf_op jit(solution)/shard_map/gather | solution.py:91
  360.2 4.3 %collective-permute-start = (bf16[128,4096]{1,0:T(8,128)(2,1)S(1)}, bf16[128,4096]{1,0:T(8,128)(2,1)S(1)}, u32[]{:S(2)}, u32[]{:S(2)}) collective-permute-start(bf16[128,4096]{1,0:T(8,128)(2,1)S(1)} %fusion.7), channel_id=1, source_target_pairs={{0,64},{64,0},{1,65},{65,1},{2,66},{66,2},{3,67},{67,3},{4,68},{68... | collective-permute-start | bytes 3145736 | tf_op jit(solution)/shard_map/ppermute | solution.py:9
  364.5 20.2 %fusion.2 = bf16[1,1,1024,4096]{3,2,1,0:T(8,128)(2,1)} fusion(bf16[64,24,1024]{2,1,0:T(8,128)(2,1)} %all-to-all-done, bf16[64,24,4096]{2,1,0:T(8,128)(2,1)} %all-to-all-done.2, f32[64,24]{1,0:T(8,128)S(1)} %bitcast.60), kind=kOutput, calls=%fused_computation.10 | convolution fusion | flops 12907970560 | bytes 24123392 | tf_op jit(solution)/shard_map/dot_general | solution.py:37
  384.7 1.0 copy.63
  (51 shorter events, 5.6 us)
Async XLA Ops:
  0.6 26.9 %copy-start = (bf16[1,128,8,1024]{3,2,1,0:T(8,128)(2,1)S(1)}, bf16[1,128,8,1024]{3,2,1,0:T(8,128)(2,1)}, u32[]{:S(2)}) copy-start(bf16[1,128,8,1024]{3,2,1,0:T(8,128)(2,1)} %param.7) | copy-start | bytes 6291460
  33.3 25.0 %copy-start.2 = (bf16[1,128,4096]{2,1,0:T(8,128)(2,1)S(1)}, bf16[1,128,4096]{2,1,0:T(8,128)(2,1)}, u32[]{:S(2)}) copy-start(bf16[1,128,4096]{2,1,0:T(8,128)(2,1)} %param.6) | copy-start | bytes 3145732
  46.1 52.2 %all-to-all-start = ((bf16[64,24,1024]{2,1,0:T(8,128)(2,1)}), bf16[64,24,1024]{2,1,0:T(8,128)(2,1)}, u32[]{:S(2)}, u32[]{:S(2)}) async-start(bf16[64,24,1024]{2,1,0:T(8,128)(2,1)} %broadcast_select_fusion.1), calls=%async_computation | async-start | bytes 6291456 | tf_op jit(solution)/shard_map/all_to_all | solution.py:76
  98.4 194.6 %all-to-all-start.2 = ((bf16[64,24,4096]{2,1,0:T(8,128)(2,1)}), bf16[64,24,4096]{2,1,0:T(8,128)(2,1)}, u32[]{:S(2)}, u32[]{:S(2)}) async-start(bf16[64,24,4096]{2,1,0:T(8,128)(2,1)} %broadcast_select_fusion), calls=%async_computation.2 | async-start | bytes 25165824 | tf_op jit(solution)/shard_map/all_to_all | solution.py:75
  292.9 41.1 %all-to-all-start.1 = ((bf16[64,1,24]{2,1,0:T(2,128)(2,1)}), bf16[64,1,24]{2,1,0:T(2,128)(2,1)S(1)}, u32[]{:S(2)}, u32[]{:S(2)}) async-start(bf16[64,1,24]{2,1,0:T(2,128)(2,1)} %all_to_all.24), calls=%async_computation.1 | async-start | bytes 65536 | tf_op jit(solution)/shard_map/all_to_all | solution.py:77
  314.3 45.3 %copy-start.4 = (f32[1,128,8]{1,2,0:T(8,128)S(1)}, f32[1,128,8]{1,2,0:T(8,128)}, u32[]{:S(2)}) copy-start(f32[1,128,8]{1,2,0:T(8,128)} %param.9) | copy-start | bytes 12292
  314.3 45.3 %copy-start.5 = (s32[1,128,8]{1,2,0:T(8,128)S(1)}, s32[1,128,8]{1,2,0:T(8,128)}, u32[]{:S(2)}) copy-start(s32[1,128,8]{1,2,0:T(8,128)} %param.8) | copy-start | bytes 12292
  314.3 45.4 %copy-start.3 = (bf16[1,64,4096]{2,1,0:T(8,128)(2,1)S(1)}, bf16[1,64,4096]{2,1,0:T(8,128)(2,1)}, u32[]{:S(2)}) copy-start(bf16[1,64,4096]{2,1,0:T(8,128)(2,1)} %param.11) | copy-start | bytes 1572868
  334.0 18.0 %all-to-all-start.3 = ((f32[64,1,24]{2,1,0:T(1,128)}), f32[64,1,24]{2,1,0:T(1,128)S(1)}, u32[]{:S(2)}, u32[]{:S(2)}) async-start(f32[64,1,24]{2,1,0:T(1,128)} %bitcast.16), calls=%async_computation.3 | async-start | bytes 65536 | tf_op jit(solution)/shard_map/all_to_all | solution.py:83
  360.2 24.6 %collective-permute-start = (bf16[128,4096]{1,0:T(8,128)(2,1)S(1)}, bf16[128,4096]{1,0:T(8,128)(2,1)S(1)}, u32[]{:S(2)}, u32[]{:S(2)}) collective-permute-start(bf16[128,4096]{1,0:T(8,128)(2,1)S(1)} %fusion.7), channel_id=1, source_target_pairs={{0,64},{64,0},{1,65},{65,1},{2,66},{66,2},{3,67},{67,3},{4,68},{68... | collective-permute-start | bytes 3145736 | tf_op jit(solution)/shard_map/ppermute | solution.py:9
  364.5 21.2 %copy-start.1 = (bf16[1,128,8,1024]{3,2,1,0:T(8,128)(2,1)S(1)}, bf16[1,128,8,1024]{3,2,1,0:T(8,128)(2,1)}, u32[]{:S(2)}) copy-start(bf16[1,128,8,1024]{3,2,1,0:T(8,128)(2,1)} %param.7) | copy-start | bytes 6291460
where the time goes:
time: 386 us
  waiting for transfers between devices  197 us (51%)
  starting transfers between devices  60.2 us (16%)
  local copies, waits for them, and re-layouts  47.7 us (12%)
  other arithmetic  40 us (10%)
  matrix products  39.7 us (10%)
    all_to_all x1, waiting for transfers between devices, body(): lax.all_to_all(grad_slots, 'expert', split_axis=0, concat_axis=0, tiled=T...  169 us
    all_to_all x1, starting transfers between devices, body(): lax.all_to_all(weight_slots, 'expert', split_axis=0, concat_axis=0, tiled...  21.3 us
    dot_general x1, matrix products, weight_pass(): lax.dot_general(hidden_in, scaled, (((0,), (0,)), ((), ())), preferred_el...  20.2 us
    all_to_all x1, waiting for transfers between devices, body(): lax.all_to_all(hidden_slots, 'expert', split_axis=0, concat_axis=0, tiled...  19.8 us
    dot_general x1, matrix products, expert_derivs(): lax.dot_general(grad_in, expert_down, (((1,), (1,)), ((), ())), preferred...  19 us
    another operation x3, other arithmetic  18.2 us
    all_to_all x1, starting transfers between devices, body(): lax.all_to_all(grad_slots, 'expert', split_axis=0, concat_axis=0, tiled=T...  12.8 us
    all_to_all x1, starting transfers between devices, body(): lax.all_to_all(hidden_slots, 'expert', split_axis=0, concat_axis=0, tiled...  12.2 us
  transfers between devices with their start and end apart: 5, of which 3 were waited for; matrix products, arithmetic and copies ran while one was open for 19% of the time, Pallas kernels for 0%

commit v1 on v0

v1 whole, which is shorter than its diff:
```python
import functools
import jax
import jax.numpy as jnp
from jax import lax
from jax.experimental import pallas as pl
from jax.experimental.pallas import tpu as pltpu
from jax.sharding import PartitionSpec as P

MESH = pl.DeviceIdType.MESH
CAP = 24
ORDERS = ((0, 1, 2), (1, 2, 0), (2, 0, 1))
STRIDE = (16, 4, 1)
GB = (11, 11, 10)
HB = (2, 3, 3)


def starts(blocks):
    return tuple(128 * sum(blocks[:i]) for i in range(len(blocks)))


def comm_kernel(grad, rt, hid, tgt, wgt, F, HR,
                gb0, gb1, gb2, sc0, sc1, sc2, ha0, ha1, ha2, hb0, hb1, hb2, hc0, hc1, hc2,
                lsem, gas, gar, gbs, gbr, gcs, gcr, gcl, has, har, hbs, hbr, hcs, hcr, hcl):
    gb, sc, ha, hb, hc = (gb0, gb1, gb2), (sc0, sc1, sc2), (ha0, ha1, ha2), (hb0, hb1, hb2), (hc0, hc1, hc2)
    e = lax.axis_index("expert")
    co = (e // 16, (e // 4) % 4, e % 4)
    gcol, hcol = starts(GB), starts(HB)

    def wrap(v):
        return lax.rem(v + 4, 4)

    def peer(axis, delta):
        c = list(co)
        c[axis] = wrap(co[axis] + delta)
        return {"expert": c[0] * 16 + c[1] * 4 + c[2]}

    def rcopy(src, dst, ss, rs, axis, delta):
        return pltpu.make_async_remote_copy(src_ref=src, dst_ref=dst, send_sem=ss, recv_sem=rs,
                                            device_id=peer(axis, delta), device_id_type=MESH)

    sends = []

    def go(cp):
        cp.start()
        sends.append(cp)
        return cp

    loads = []
    for p, (A, B, C) in enumerate(ORDERS):
        gw = GB[p] * 128
        own = gb[p].at[co[B], co[A]]
        l0 = pltpu.make_async_copy(grad.at[:, pl.ds(gcol[p], gw)], own.at[:, pl.ds(0, gw)], lsem.at[p, 0])
        l1 = pltpu.make_async_copy(rt, own.at[:, pl.ds(gw, 128)], lsem.at[p, 1])
        l0.start(); l1.start()
        loads.append((l0, l1))

    def ring(p, axis, slot_of, sems, semr, idx):
        gw = GB[p] * 128 + 128
        half = (gw // 256) * 128
        def cp(i, src_delta, cols, delta):
            ref = slot_of(src_delta)
            if cols is not None:
                ref = ref.at[:, pl.ds(*cols)]
            return rcopy(ref, ref, sems.at[idx + (i,)], semr.at[idx + (i,)], axis, delta)
        return (cp(0, 0, None, 1), cp(1, 0, None, -1), cp(2, -1, (0, half), 1), cp(3, 1, (half, gw - half), -1))

    acp, bcp = [], {}
    for p, (A, B, C) in enumerate(ORDERS):
        acp.append(ring(p, A, lambda d, p=p, A=A, B=B: gb[p].at[co[B], wrap(co[A] + d)], gas, gar, (p,)))
        for k, da in enumerate((0, -1, 1, 2)):
            bcp[p, k] = ring(p, B, lambda d, p=p, A=A, B=B, da=da: gb[p].at[wrap(co[B] + d), wrap(co[A] + da)], gbs, gbr, (p, k))
    for p in range(3):
        loads[p][0].wait(); loads[p][1].wait()
        go(acp[p][0]); go(acp[p][1])
    for p in range(3):
        go(bcp[p, 0][0]); go(bcp[p, 0][1])

    for p, (A, B, C) in enumerate(ORDERS):
        hw = HB[p] * 128
        r = lax.broadcasted_iota(jnp.int32, (16 * CAP, 1), 0)
        dB = (r >= 4 * CAP).astype(jnp.int32) + (r >= 8 * CAP).astype(jnp.int32) + (r >= 12 * CAP).astype(jnp.int32)
        r1 = r - dB * (4 * CAP)
        dC = (r1 >= CAP).astype(jnp.int32) + (r1 >= 2 * CAP).astype(jnp.int32) + (r1 >= 3 * CAP).astype(jnp.int32)
        slot = r1 - dC * CAP
        base = CAP * (dB * STRIDE[B] + dC * STRIDE[C]) + slot
        for d in (1, 3, 2, 0):
            code = base + CAP * STRIDE[A] * wrap(co[A] + d)
            pick = jnp.where(code == tgt[...], wgt[...], 0.0).astype(jnp.bfloat16)
            rows = jnp.dot(pick, hid[:, hcol[p]:hcol[p] + hw], preferred_element_type=jnp.float32)
            rows = rows.reshape(4, 4, CAP, hw).astype(jnp.bfloat16)
            if d == 0:
                for j in range(4):
                    hb[p][j, co[A]] = rows[j]
            else:
                ha[p][d - 1] = rows
                go(rcopy(ha[p].at[d - 1], hb[p].at[:, co[A]], has.at[p, d - 1], har.at[p, d - 1], A, d))
    hacp = {}
    for p, (A, B, C) in enumerate(ORDERS):
        for d in (1, 2, 3):
            hacp[p, d] = rcopy(ha[p].at[d - 1], hb[p].at[:, wrap(co[A] - d)], has.at[p, d - 1], har.at[p, d - 1], A, d)

    for p in range(3):
        acp[p][0].wait_recv(); go(acp[p][2])
        acp[p][1].wait_recv(); go(acp[p][3])
    for p in range(3):
        for k in (1, 2):
            go(bcp[p, k][0]); go(bcp[p, k][1])
    for p in range(3):
        acp[p][2].wait_recv(); acp[p][3].wait_recv()
        go(bcp[p, 3][0]); go(bcp[p, 3][1])

    j = lax.broadcasted_iota(jnp.int32, (4 * CAP, 1), 0)
    dCj = (j >= CAP).astype(jnp.int32) + (j >= 2 * CAP).astype(jnp.int32) + (j >= 3 * CAP).astype(jnp.int32)
    slotj = (j - dCj * CAP).astype(jnp.float32)
    lane = lax.broadcasted_iota(jnp.int32, (4 * CAP, 64), 1)

    def pack(p, db):
        A, B, C = ORDERS[p]
        gw = GB[p] * 128
        cc = co[C] + dCj
        cc = jnp.where(cc >= 4, cc - 4, cc)
        eid = STRIDE[A] * co[A] + STRIDE[B] * co[B] + STRIDE[C] * cc
        E = jnp.where(lane == eid, 1.0, 0.0).astype(jnp.bfloat16)
        bb = wrap(co[B] + db)

        def one(a, carry):
            codes = jnp.dot(E, gb[p][bb, a, 0:64, gw:gw + 128], preferred_element_type=jnp.float32)
            sel = jnp.where(codes == slotj, 1.0, 0.0).astype(jnp.bfloat16)
            rows = jnp.dot(sel, gb[p][bb, a, :, 0:gw], preferred_element_type=jnp.float32)
            rows = rows.reshape(4, CAP, gw).astype(jnp.bfloat16)
            for dc in range(4):
                sc[p][dc, db % 4, a] = rows[dc]
            return carry
        lax.fori_loop(0, 4, one, 0)
        for dc in (1, 3, 2):
            go(rcopy(sc[p].at[dc, db % 4], fdst(p, bb, 0), gcs.at[p, db % 4, dc - 1], gcr.at[p, db % 4, dc - 1], C, dc))
        cp = pltpu.make_async_copy(sc[p].at[0, db % 4], fdst(p, bb, 0), gcl.at[p, db % 4])
        cp.start()
        locals_.append(cp)

    def fdst(p, bb, d):
        A, B, C = ORDERS[p]
        idx = [None, None, None]
        idx[A] = slice(None)
        idx[B] = bb
        idx[C] = wrap(co[C] - d)
        return F.at[idx[0], idx[1], idx[2], :, pl.ds(gcol[p], GB[p] * 128)]

    def hdst(p, bb, d):
        A, B, C = ORDERS[p]
        idx = [None, None, None]
        idx[A] = slice(None)
        idx[B] = bb
        idx[C] = wrap(co[C] - d)
        return HR.at[idx[0], idx[1], idx[2], :, pl.ds(hcol[p], HB[p] * 128)]

    locals_ = []
    hbcp = {}
    for p, (A, B, C) in enumerate(ORDERS):
        for d in (1, 3, 2):
            hacp[p, d].wait_recv()
        for d in (1, 3, 2):
            hbcp[p, d] = go(rcopy(hb[p].at[wrap(co[B] + d)], hc[p].at[d - 1], hbs.at[p, d - 1], hbr.at[p, d - 1], B, d))
    for p in range(3):
        pack(p, 0)
    for k in range(4):
        for p in range(3):
            bcp[p, k][0].wait_recv(); go(bcp[p, k][2])
            bcp[p, k][1].wait_recv(); go(bcp[p, k][3])

    def hidden_c(p, d):
        A, B, C = ORDERS[p]
        bb = wrap(co[B] - d)
        for dc in (1, 3, 2, 0):
            cs = wrap(co[C] + dc)
            src = hb[p].at[co[B], :, cs] if d == 0 else hc[p].at[d - 1, :, cs]
            if dc == 0:
                cp = pltpu.make_async_copy(src, hdst(p, bb, 0), hcl.at[p, d])
                cp.start()
                locals_.append(cp)
            else:
                go(rcopy(src, hdst(p, bb, 0), hcs.at[p, d, dc - 1], hcr.at[p, d, dc - 1], C, dc))
    for p in range(3):
        hidden_c(p, 0)
    for p in range(3):
        pack(p, -1)
    for p in range(3):
        pack(p, 1)
    for p in range(3):
        for d in (1, 3, 2):
            hbcp[p, d].wait_recv()
            hidden_c(p, d)
    for p in range(3):
        for k in range(4):
            bcp[p, k][2].wait_recv(); bcp[p, k][3].wait_recv()
        pack(p, 2)
    for p, (A, B, C) in enumerate(ORDERS):
        for db in (0, -1, 1, 2):
            bb = wrap(co[B] + db)
            for dc in (1, 3, 2):
                rcopy(sc[p].at[dc, db % 4], fdst(p, bb, dc), gcs.at[p, db % 4, dc - 1], gcr.at[p, db % 4, dc - 1], C, dc).wait_recv()
        for d in range(4):
            for dc in (1, 3, 2):
                src = hc[p].at[max(d - 1, 0), :, 0]
                rcopy(src, hdst(p, wrap(co[B] - d), dc), hcs.at[p, d, dc - 1], hcr.at[p, d, dc - 1], C, dc).wait_recv()
    for cp in locals_:
        cp.wait()
    for cp in sends:
        cp.wait_send()


def exchange(grad, rt, hid, tgt, wgt):
    bf = jnp.bfloat16
    V = pltpu.VMEM
    D = pltpu.SemaphoreType.DMA
    any_ = pl.BlockSpec(memory_space=pl.ANY)
    vm = pl.BlockSpec(memory_space=pltpu.VMEM)
    F, HR = pl.pallas_call(
        comm_kernel,
        out_shape=(jax.ShapeDtypeStruct((4, 4, 4, CAP, 4096), bf), jax.ShapeDtypeStruct((4, 4, 4, CAP, 1024), bf)),
        in_specs=[any_, any_, vm, vm, vm], out_specs=(any_, any_),
        scratch_shapes=[V((4, 4, 128, g * 128 + 128), bf) for g in GB]
        + [V((4, 4, 4, CAP, g * 128), bf) for g in GB]
        + [V((3, 4, 4, CAP, h * 128), bf) for h in HB]
        + [V((4, 4, 4, CAP, h * 128), bf) for h in HB]
        + [V((3, 4, 4, CAP, h * 128), bf) for h in HB]
        + [D((3, 2)), D((3, 4)), D((3, 4)), D((3, 4, 4)), D((3, 4, 4)), D((3, 4, 3)), D((3, 4, 3)), D((3, 4)),
           D((3, 3)), D((3, 3)), D((3, 3)), D((3, 3)), D((3, 4, 3)), D((3, 4, 3)), D((3, 4))],
        compiler_params=pltpu.CompilerParams(has_side_effects=True, vmem_limit_bytes=62 * 2**20),
    )(grad, rt, hid, tgt, wgt)
    return F.reshape(64 * CAP, 4096), HR.reshape(64 * CAP, 1024)


def body(grad_out, saved_hidden, routes, scores, down_weight, router):
    grad_rows, route_ids, score_rows = grad_out[0], routes[0], scores[0]
    expert_down, router_rows = down_weight[0, 0], router[0]
    n_tokens, n_routes, hidden_width = saved_hidden.shape[1:]
    n_experts = router_rows.shape[0]
    hidden_flat = saved_hidden[0].reshape(n_tokens * n_routes, hidden_width)
    ids = jnp.arange(n_experts, dtype=jnp.int32)
    onehot = (route_ids[:, :, None] == ids).astype(jnp.float32)
    member = jnp.sum(onehot, axis=1)
    t = jnp.arange(n_tokens, dtype=jnp.int32)
    tril = (t[:, None] > t[None, :]).astype(jnp.bfloat16)
    rank = jnp.dot(tril, member.astype(jnp.bfloat16), preferred_element_type=jnp.float32)
    code = jnp.where(member > 0, rank, -1.0)
    rt = jnp.zeros((128, 128), jnp.bfloat16).at[:n_experts].set(code.T.astype(jnp.bfloat16))
    slot = jnp.sum(onehot * rank[:, None, :], axis=2).astype(jnp.int32)
    target = route_ids * CAP + slot
    total = jnp.sum(score_rows, axis=1, keepdims=True)
    weights = score_rows / total
    low = weights.astype(jnp.bfloat16).astype(jnp.float32)
    grad_recv, hidden_recv = exchange(grad_rows, rt, hidden_flat, target.reshape(1, -1), low.reshape(1, -1))
    proj = lax.dot_general(grad_recv, expert_down, (((1,), (1,)), ((), ())), preferred_element_type=jnp.float32)
    derivs = jnp.sum(proj * hidden_recv.astype(jnp.float32), axis=1)
    back = lax.all_to_all(derivs.reshape(n_experts, CAP), "expert", split_axis=0, concat_axis=0, tiled=True)
    weight_out = lax.dot_general(hidden_recv, grad_recv, (((0,), (0,)), ((), ())), preferred_element_type=jnp.float32).astype(jnp.bfloat16)
    home = jnp.zeros((n_tokens, n_experts), jnp.float32)
    for s in range(CAP):
        home = home + jnp.where(code == s, back[:, s][None, :], 0.0)
    rd = jnp.sum(onehot * home[:, None, :], axis=2) / low
    center = jnp.sum(weights * rd, axis=1, keepdims=True)
    logit = score_rows * (1.0 - score_rows) / total * (rd - center)
    dense = jnp.sum(onehot * logit[:, :, None], axis=1)
    inp = grad_rows.astype(jnp.float32) + jnp.dot(dense, router_rows.astype(jnp.float32))
    handed = lax.ppermute(inp.astype(jnp.bfloat16), "section", [(0, 1), (1, 0)])
    return weight_out[None, None], handed[None]


def solution(mesh):
    return jax.shard_map(
        body, mesh=mesh,
        in_specs=(P("section", "expert", None), P("section", "expert", None, None), P("section", "expert", None),
                  P("section", "expert", None), P("section", "expert", None, None), P("section", None, None)),
        out_specs=(P("section", "expert", None, None), P("section", "expert", None)), check_vma=False)
```

time: 386 us -> 243 us (0.63)
  waiting for transfers between devices: 197 us -> 0.01 us
  Pallas kernels: 0 us -> 162 us
  starting transfers between devices: 60.2 us -> 2.48 us
  local copies, waits for them, and re-layouts: 47.7 us -> 10.6 us
  other arithmetic: 40 us -> 9.85 us
  blocking collectives: 0 us -> 17.4 us
    all_to_all x4 -> x0, waiting for transfers between devices: 197 us -> none  [the longest x1 169 us: body(): lax.all_to_all(grad_slots, 'expert', split_axis=0, concat_axis=0, tiled=T...]
    pallas_call x0 -> x1, Pallas kernels: none -> 162 us  [exchange(): pl.pallas_call(comm_kernel, out_shape=(jax.ShapeDtypeStruct((4, 4, 4, CAP...]
    all_to_all x4 -> x0, starting transfers between devices: 55.9 us -> none  [the longest x1 21.3 us: body(): lax.all_to_all(weight_slots, 'expert', split_axis=0, concat_axis=0, tiled...]
    gather x4 -> x0, local copies, waits for them, and re-layouts: 30.9 us -> none  [the longest x1 9.54 us: body(): grad_rows[safe_index // n_routes]]
    another operation x3 -> x0, other arithmetic: 18.2 us -> none
    all_to_all x0 -> x1, blocking collectives: none -> 17.4 us  [body(): lax.all_to_all(derivs.reshape(n_experts, CAP), 'expert', split_axis=0, co...]
    select_n x5 -> x0, other arithmetic: 14 us -> none  [the longest x1 10.7 us: body(): jnp.where(filled[:, None], grad_rows[safe_index // n_routes], jnp.zeros((...]
    dot_general x3 -> x4, matrix products: 39.7 us -> 38.9 us  [the longest x1 19.3 us: body(): lax.dot_general(hidden_recv, grad_recv, (((0,), (0,)), ((), ())), preferr...]
  transfers between devices with their start and end apart: 5 -> 1, of which waited for: 3 -> 0; matrix products, arithmetic and copies ran while one was open for 19% -> 8% of each run, Pallas kernels for 0% -> 0%
where the time goes in v1:
time: 243 us; the launch traced here: 242 us
  Pallas kernels  162 us (67%)
  matrix products  38.9 us (16%)
  blocking collectives  17.4 us (7%)
  local copies, waits for them, and re-layouts  10.6 us (4%)
  other arithmetic  9.85 us (4%)
  starting transfers between devices  2.48 us (1%)
    pallas_call x1, Pallas kernels, exchange(): pl.pallas_call(comm_kernel, out_shape=(jax.ShapeDtypeStruct((4, 4, 4, CAP...  162 us
    dot_general x1, matrix products, body(): lax.dot_general(hidden_recv, grad_recv, (((0,), (0,)), ((), ())), preferr...  19.3 us
    dot_general x1, matrix products, body(): lax.dot_general(grad_recv, expert_down, (((1,), (1,)), ((), ())), preferr...  19 us
    all_to_all x1, blocking collectives, body(): lax.all_to_all(derivs.reshape(n_experts, CAP), 'expert', split_axis=0, co...  17.4 us
    convert_element_type x1, local copies, waits for them, and re-layouts, body(): derivs = jnp.sum(proj * hidden_recv.astype(jnp.float32), axis=1)  6.59 us
    convert_element_type x1, other arithmetic, body(): derivs = jnp.sum(proj * hidden_recv.astype(jnp.float32), axis=1)  5.34 us
  transfers between devices with their start and end apart: 1, of which 0 were waited for; matrix products, arithmetic and copies ran while one was open for 8% of the time, Pallas kernels for 0%

profile of v1, /device:TPU:1, one launch (start us, length us, event | category | flops | bytes accessed | tf_op | source)
XLA Modules:
  0.0 242.5 jit_solution(11027749861984468022)
XLA Ops:
  0.6 0.7 broadcast_multiply_fusion
  1.4 0.7 convert_reduce_fusion
  2.1 0.1 fusion.7
  2.3 0.7 select_reduce_fusion.2
  3.0 0.8 copy.43
  3.8 0.7 reduce_sum.65
  4.5 0.1 copy.42
  4.7 0.1 copy.41
  5.0 0.1 div.41
  5.2 0.6 scatter.4.rt
  5.8 0.6 add.86.tgt
  6.4 0.6 convert_convert_fusion.wgt
  7.0 162.5 %shard_map.77 = (bf16[4,4,4,24,4096]{4,3,2,1,0:T(8,128)(2,1)}, bf16[4,4,4,24,1024]{4,3,2,1,0:T(8,128)(2,1)}) custom-call(bf16[128,4096]{1,0:T(8,128)(2,1)} %bitcast.42, bf16[128,128]{1,0:T(8,128)(2,1)} %scatter.4.rt, bf16[1024,1024]{1,0:T(8,128)(2,1)} %bitcast.43, s32[1,1024]{1,0:T(1,128)} %add.86.tgt, f32[1,1024]{1,0:T(1,128)} %convert_convert_fusion.wgt), custom_call_target="tpu_custom_call" | custom-call | tf_op jit(solution)/shard_map/pallas_call | solution.py:218
  169.5 5.3 %bitcast_convert_fusion.1 = f32[1536,1024]{1,0:T(8,128)} fusion(bf16[4,4,4,24,1024]{4,3,2,1,0:T(8,128)(2,1)} %get-tuple-element.16), kind=kLoop, calls=%fused_computation.7 | loop fusion | flops 1572864 | bytes 9437184 | tf_op jit(solution)/shard_map/convert_element_type | solution.py:255
  174.8 6.6 %copy.45 = f32[1536,1024]{0,1:T(8,128)} copy(f32[1536,1024]{1,0:T(8,128)} %bitcast_convert_fusion.1) | data formatting | bytes 12582912 | tf_op jit(solution)/shard_map/convert_element_type | solution.py:255
  181.4 19.0 %multiply_reduce_fusion = f32[1536]{0:T(1024)S(1)} fusion(f32[1536,1024]{0,1:T(8,128)} %copy.45, bf16[1536,4096]{1,0:T(8,128)(2,1)} %bitcast.50, bf16[1,1,1024,4096]{3,2,1,0:T(8,128)(2,1)} %param.12), kind=kOutput, calls=%fused_computation.4 | convolution fusion | flops 12888045568 | bytes 27269120 | tf_op jit(solution)/shard_map/dot_general | solution.py:254
  200.5 17.4 %all_to_all.12 = f32[64,1,24]{2,1,0:T(1,128)S(1)} all-to-all(f32[64,1,24]{2,1,0:T(1,128)S(1)} %bitcast.45), channel_id=1, replica_groups=mesh['section'=2,'expert'=64] {'expert'}, dimensions={0} | all-to-all | bytes 12288 | tf_op jit(solution)/shard_map/all_to_all | solution.py:256
  217.9 0.3 slice_reduce_fusion.22
  218.2 0.6 slice_reduce_fusion.23
  218.8 0.3 select_add_fusion
  219.3 0.5 fusion.5
  219.7 2.5 %collective-permute-start = (bf16[128,4096]{1,0:T(8,128)(2,1)S(1)}, bf16[128,4096]{1,0:T(8,128)(2,1)S(1)}, u32[]{:S(2)}, u32[]{:S(2)}) collective-permute-start(bf16[128,4096]{1,0:T(8,128)(2,1)S(1)} %fusion.5), channel_id=1, source_target_pairs={{0,64},{64,0},{1,65},{65,1},{2,66},{66,2},{3,67},{67,3},{4,68},{68... | collective-permute-start | bytes 3145736 | tf_op jit(solution)/shard_map/ppermute | solution.py:266
  222.2 19.3 %fusion.2 = bf16[1,1,1024,4096]{3,2,1,0:T(8,128)(2,1)} fusion(bf16[4,4,4,24,1024]{4,3,2,1,0:T(8,128)(2,1)} %get-tuple-element.16, bf16[4,4,4,24,4096]{4,3,2,1,0:T(8,128)(2,1)} %get-tuple-element.17), kind=kOutput, calls=%fused_computation.3 | convolution fusion | flops 12889096192 | bytes 24117248 | tf_op jit(solution)/shard_map/dot_general | solution.py:257
  241.5 1.0 copy.49
  (20 shorter events, 0.6 us)
Async XLA Ops:
  0.6 218.6 %copy-start = (bf16[1,64,4096]{2,1,0:T(8,128)(2,1)S(1)}, bf16[1,64,4096]{2,1,0:T(8,128)(2,1)}, u32[]{:S(2)}) copy-start(bf16[1,64,4096]{2,1,0:T(8,128)(2,1)} %param.13) | copy-start | bytes 1572868
  181.4 37.7 %copy-start.2 = (s32[1,128,8]{1,2,0:T(8,128)S(1)}, s32[1,128,8]{1,2,0:T(8,128)}, u32[]{:S(2)}) copy-start(s32[1,128,8]{1,2,0:T(8,128)} %param.10) | copy-start | bytes 12292
  181.4 37.7 %copy-start.3 = (f32[1,128,8]{1,2,0:T(8,128)S(1)}, f32[1,128,8]{1,2,0:T(8,128)}, u32[]{:S(2)}) copy-start(f32[1,128,8]{1,2,0:T(8,128)} %param.11) | copy-start | bytes 12292
  181.4 37.8 %copy-start.1 = (bf16[1,128,4096]{2,1,0:T(8,128)(2,1)S(1)}, bf16[1,128,4096]{2,1,0:T(8,128)(2,1)}, u32[]{:S(2)}) copy-start(bf16[1,128,4096]{2,1,0:T(8,128)(2,1)} %param.8) | copy-start | bytes 3145732
  219.7 21.8 %collective-permute-start = (bf16[128,4096]{1,0:T(8,128)(2,1)S(1)}, bf16[128,4096]{1,0:T(8,128)(2,1)S(1)}, u32[]{:S(2)}, u32[]{:S(2)}) collective-permute-start(bf16[128,4096]{1,0:T(8,128)(2,1)S(1)} %fusion.5), channel_id=1, source_target_pairs={{0,64},{64,0},{1,65},{65,1},{2,66},{66,2},{3,67},{67,3},{4,68},{68... | collective-permute-start | bytes 3145736 | tf_op jit(solution)/shard_map/ppermute | solution.py:266

commit v2 on v1

--- a/solution.py
+++ b/solution.py
@@ -10,7 +10,7 @@
 CAP = 24
 ORDERS = ((0, 1, 2), (1, 2, 0), (2, 0, 1))
 STRIDE = (16, 4, 1)
-GB = (11, 11, 10)
+GB = (10, 12, 10)
 HB = (2, 3, 3)
 
 
@@ -18,9 +18,9 @@
     return tuple(128 * sum(blocks[:i]) for i in range(len(blocks)))
 
 
-def comm_kernel(grad, rt, hid, tgt, wgt, F, HR,
+def comm_kernel(routes, scores, router, grad, hidden, down, F, HR, handed, hid, HV, wv, gch, g2, ds, dr, hnd, codes_s, score_s,
                 gb0, gb1, gb2, sc0, sc1, sc2, ha0, ha1, ha2, hb0, hb1, hb2, hc0, hc1, hc2,
-                lsem, gas, gar, gbs, gbr, gcs, gcr, gcl, has, har, hbs, hbr, hcs, hcr, hcl):
+                lsem, gas, gar, gbs, gbr, gcs, gcr, gcl, has, har, hbs, hbr, hcs, hcr, gls, wsem, dss, drs, hos, hns, hnr):
     gb, sc, ha, hb, hc = (gb0, gb1, gb2), (sc0, sc1, sc2), (ha0, ha1, ha2), (hb0, hb1, hb2), (hc0, hc1, hc2)
     e = lax.axis_index("expert")
     co = (e // 16, (e // 4) % 4, e % 4)
@@ -50,9 +50,33 @@
         gw = GB[p] * 128
         own = gb[p].at[co[B], co[A]]
         l0 = pltpu.make_async_copy(grad.at[:, pl.ds(gcol[p], gw)], own.at[:, pl.ds(0, gw)], lsem.at[p, 0])
-        l1 = pltpu.make_async_copy(rt, own.at[:, pl.ds(gw, 128)], lsem.at[p, 1])
-        l0.start(); l1.start()
-        loads.append((l0, l1))
+        l0.start()
+        loads.append(l0)
+    hload = pltpu.make_async_copy(hidden, hid, lsem.at[0, 1])
+    hload.start()
+    wload = pltpu.make_async_copy(down, wv, wsem.at[0])
+    wload.start()
+
+    f32, bf = jnp.float32, jnp.bfloat16
+    ri = jnp.transpose(routes[...].astype(f32))
+    st = jnp.transpose(scores[...])
+    tot = jnp.sum(st, axis=0, keepdims=True)
+    low = (st / tot).astype(bf)
+    eio = lax.broadcasted_iota(jnp.int32, (64, 128), 0).astype(f32)
+    member = jnp.zeros((64, 128), f32)
+    score_e = jnp.zeros((64, 128), f32)
+    for k in range(8):
+        hit = eio == ri[k:k + 1, :]
+        member = member + jnp.where(hit, 1.0, 0.0)
+        score_e = score_e + jnp.where(hit, st[k:k + 1, :], 0.0)
+    before = lax.broadcasted_iota(jnp.int32, (128, 128), 0) < lax.broadcasted_iota(jnp.int32, (128, 128), 1)
+    rank = jnp.dot(member.astype(bf), jnp.where(before, 1.0, 0.0).astype(bf), preferred_element_type=f32)
+    code_e = jnp.where(member > 0.0, rank, -1.0)
+    codes_s[...] = code_e
+    score_s[...] = score_e
+    code_b = jnp.concatenate([code_e, jnp.full((64, 128), -1.0, f32)], axis=0).astype(bf)
+    for p, (A, B, C) in enumerate(ORDERS):
+        gb[p][co[B], co[A], :, GB[p] * 128:GB[p] * 128 + 128] = code_b
 
     def ring(p, axis, slot_of, sems, semr, idx):
         gw = GB[p] * 128 + 128
@@ -70,10 +94,21 @@
         for k, da in enumerate((0, -1, 1, 2)):
             bcp[p, k] = ring(p, B, lambda d, p=p, A=A, B=B, da=da: gb[p].at[wrap(co[B] + d), wrap(co[A] + da)], gbs, gbr, (p, k))
     for p in range(3):
-        loads[p][0].wait(); loads[p][1].wait()
+        loads[p].wait()
         go(acp[p][0]); go(acp[p][1])
     for p in range(3):
         go(bcp[p, 0][0]); go(bcp[p, 0][1])
+
+    slots = jnp.concatenate([jnp.sum(jnp.where(eio == ri[k:k + 1, :], rank, 0.0), axis=0, keepdims=True) for k in range(8)], axis=0)
+    n8 = lax.broadcasted_iota(jnp.int32, (128, 1024), 1) // 8
+    spread = jnp.where(n8 == lax.broadcasted_iota(jnp.int32, (128, 1024), 0), 1.0, 0.0).astype(bf)
+    mine = lax.broadcasted_iota(jnp.int32, (8, 1024), 1) % 8 == lax.broadcasted_iota(jnp.int32, (8, 1024), 0)
+
+    def lanes(v):
+        return jnp.sum(jnp.where(mine, jnp.dot(v.astype(bf), spread, preferred_element_type=f32), 0.0), axis=0, keepdims=True)
+    tgt = CAP * lanes(ri) + lanes(slots)
+    wgt = lanes(low)
+    hload.wait()
 
     for p, (A, B, C) in enumerate(ORDERS):
         hw = HB[p] * 128
@@ -85,7 +120,7 @@
         base = CAP * (dB * STRIDE[B] + dC * STRIDE[C]) + slot
         for d in (1, 3, 2, 0):
             code = base + CAP * STRIDE[A] * wrap(co[A] + d)
-            pick = jnp.where(code == tgt[...], wgt[...], 0.0).astype(jnp.bfloat16)
+            pick = jnp.where(code.astype(f32) == tgt, wgt, 0.0).astype(jnp.bfloat16)
             rows = jnp.dot(pick, hid[:, hcol[p]:hcol[p] + hw], preferred_element_type=jnp.float32)
             rows = rows.reshape(4, 4, CAP, hw).astype(jnp.bfloat16)
             if d == 0:
@@ -136,7 +171,7 @@
             go(rcopy(sc[p].at[dc, db % 4], fdst(p, bb, 0), gcs.at[p, db % 4, dc - 1], gcr.at[p, db % 4, dc - 1], C, dc))
         cp = pltpu.make_async_copy(sc[p].at[0, db % 4], fdst(p, bb, 0), gcl.at[p, db % 4])
         cp.start()
-        locals_.append(cp)
+        locals_[p, db % 4] = cp
 
     def fdst(p, bb, d):
         A, B, C = ORDERS[p]
@@ -152,9 +187,9 @@
         idx[A] = slice(None)
         idx[B] = bb
         idx[C] = wrap(co[C] - d)
-        return HR.at[idx[0], idx[1], idx[2], :, pl.ds(hcol[p], HB[p] * 128)]
-
-    locals_ = []
+        return HV.at[idx[0], idx[1], idx[2], :, pl.ds(hcol[p], HB[p] * 128)]
+
+    locals_ = {}
     hbcp = {}
     for p, (A, B, C) in enumerate(ORDERS):
         for d in (1, 3, 2):
@@ -175,9 +210,9 @@
             cs = wrap(co[C] + dc)
             src = hb[p].at[co[B], :, cs] if d == 0 else hc[p].at[d - 1, :, cs]
             if dc == 0:
-                cp = pltpu.make_async_copy(src, hdst(p, bb, 0), hcl.at[p, d])
-                cp.start()
-                locals_.append(cp)
+                dst = hdst(p, bb, 0)
+                for a in range(4):
+                    dst[a] = src[a]
             else:
                 go(rcopy(src, hdst(p, bb, 0), hcs.at[p, d, dc - 1], hcr.at[p, d, dc - 1], C, dc))
     for p in range(3):
@@ -195,75 +230,146 @@
             bcp[p, k][2].wait_recv(); bcp[p, k][3].wait_recv()
         pack(p, 2)
     for p, (A, B, C) in enumerate(ORDERS):
-        for db in (0, -1, 1, 2):
-            bb = wrap(co[B] + db)
-            for dc in (1, 3, 2):
-                rcopy(sc[p].at[dc, db % 4], fdst(p, bb, dc), gcs.at[p, db % 4, dc - 1], gcr.at[p, db % 4, dc - 1], C, dc).wait_recv()
         for d in range(4):
             for dc in (1, 3, 2):
                 src = hc[p].at[max(d - 1, 0), :, 0]
                 rcopy(src, hdst(p, wrap(co[B] - d), dc), hcs.at[p, d, dc - 1], hcr.at[p, d, dc - 1], C, dc).wait_recv()
-    for cp in locals_:
-        cp.wait()
+    hout = pltpu.make_async_copy(HV, HR, hos.at[0])
+    hout.start()
+    wload.wait()
+
+    def rest(p):
+        return tuple(ax for ax in range(3) if ax != ORDERS[p][1])
+
+    def at_b(ref, p, bb):
+        idx = [slice(None)] * 3
+        idx[ORDERS[p][1]] = bb
+        return ref.at[idx[0], idx[1], idx[2]]
+
+    chunks = [(p, db) for db in (0, -1, 1, 2) for p in range(3)]
+
+    def load(n):
+        p, db = chunks[n]
+        C = ORDERS[p][2]
+        bb = wrap(co[ORDERS[p][1]] + db)
+        for dc in (1, 3, 2):
+            rcopy(sc[p].at[dc, db % 4], fdst(p, bb, dc), gcs.at[p, db % 4, dc - 1], gcr.at[p, db % 4, dc - 1], C, dc).wait_recv()
+        locals_[p, db % 4].wait()
+        gw = GB[p] * 128
+        cp = pltpu.make_async_copy(at_b(F, p, bb).at[:, :, :, pl.ds(gcol[p], gw)], gch.at[n % 2, :, :, :, pl.ds(0, gw)], gls.at[n % 2])
+        cp.start()
+        return cp
+
+    def derive(n):
+        p, db = chunks[n]
+        gw = GB[p] * 128
+        B = ORDERS[p][1]
+        bb = wrap(co[B] + db)
+        R1, R2 = rest(p)
+        for i in range(4):
+            g2[i * 96:(i + 1) * 96, 0:gw] = gch[n % 2, i, :, :, 0:gw].astype(f32).reshape(96, gw).astype(bf)
+        hview = at_b(HV, p, bb)
+        acc = jnp.zeros((384, 128), f32)
+        for f in range(4):
+            proj = lax.dot_general(g2[:, 0:gw], wv[f * 256:(f + 1) * 256, gcol[p]:gcol[p] + gw], (((1,), (1,)), ((), ())),
+                                   preferred_element_type=f32)
+            q = proj * hview[:, :, :, f * 256:(f + 1) * 256].astype(f32).reshape(384, 256)
+            acc = acc + q[:, 0:128] + q[:, 128:256]
+        pad = jnp.concatenate([acc.reshape(16, CAP, 128), jnp.zeros((16, 8, 128), f32)], axis=1).reshape(512, 128)
+        row = jnp.sum(jnp.transpose(pad), axis=0, keepdims=True)
+        for i in range(4):
+            ds[p, db % 4, i] = row[:, i * 128:(i + 1) * 128]
+        for d1 in range(4):
+            for d2 in range(4):
+                i = wrap(co[R1] + d1)
+                if (db, d1, d2) == (0, 0, 0):
+                    dr[p, e] = ds[p, 0, i]
+                    continue
+                c = [None] * 3
+                c[R1], c[R2], c[B] = i, wrap(co[R2] + d2), bb
+                pltpu.make_async_remote_copy(src_ref=ds.at[p, db % 4, i], dst_ref=dr.at[p, e], send_sem=dss.at[p], recv_sem=drs.at[p],
+                                             device_id={"expert": c[0] * 16 + c[1] * 4 + c[2]}, device_id_type=MESH).start()
+
+    cur = load(0)
+    for n in range(12):
+        nxt = load(n + 1) if n < 11 else None
+        cur.wait()
+        derive(n)
+        cur = nxt
+
+    home = jnp.zeros((64, 128), f32)
+    window = lax.broadcasted_iota(jnp.int32, (64, 128), 1) // 32
+    for p in range(3):
+        pltpu.make_async_copy(dr.at[p, pl.ds(0, 63)], dr.at[p, pl.ds(0, 63)], drs.at[p]).wait()
+        home = home + jnp.where(window == co[rest(p)[1]], dr[p].reshape(64, 128), 0.0)
+    home = home + pltpu.roll(home, 64, 1)
+    home = home + pltpu.roll(home, 32, 1)
+    code_e = codes_s[...]
+    score_e = score_s[...]
+    rd = jnp.zeros((64, 128), f32)
+    for s in range(CAP):
+        rd = rd + jnp.where(code_e == float(s), home[:, s:s + 1], 0.0)
+    tot = jnp.sum(score_e, axis=0, keepdims=True)
+    weight = score_e / tot
+    on = code_e >= 0.0
+    rd = jnp.where(on, rd / jnp.where(on, weight.astype(bf).astype(f32), 1.0), 0.0)
+    center = jnp.sum(weight * rd, axis=0, keepdims=True)
+    logit = score_e * (1.0 - score_e) / tot * (rd - center)
+    lt = jnp.transpose(logit).astype(bf)
+    other = {"section": 1 - lax.axis_index("section")}
+    hcps = []
+    for p, (A, B, C) in enumerate(ORDERS):
+        gw = GB[p] * 128
+        for c0 in range(0, gw, 256):
+            add = jnp.dot(lt, router[:, gcol[p] + c0:gcol[p] + c0 + 256], preferred_element_type=f32)
+            hnd[:, gcol[p] + c0:gcol[p] + c0 + 256] = (gb[p][co[B], co[A], :, c0:c0 + 256].astype(f32) + add).astype(bf)
+        cols = pl.ds(gcol[p], gw)
+        cp = pltpu.make_async_remote_copy(src_ref=hnd.at[:, cols], dst_ref=handed.at[:, cols], send_sem=hns.at[p], recv_sem=hnr.at[p],
+                                          device_id=other, device_id_type=MESH)
+        cp.start()
+        hcps.append(cp)
+    for p in range(3):
+        pltpu.make_async_copy(dr.at[p, pl.ds(0, 63)], dr.at[p, pl.ds(0, 63)], dss.at[p]).wait()
+    hout.wait()
     for cp in sends:
         cp.wait_send()
-
-
-def exchange(grad, rt, hid, tgt, wgt):
-    bf = jnp.bfloat16
+    for cp in hcps:
+        cp.wait()
+
+
+def exchange(routes, scores, router, grad, hidden, down):
+    bf, f32 = jnp.bfloat16, jnp.float32
     V = pltpu.VMEM
     D = pltpu.SemaphoreType.DMA
     any_ = pl.BlockSpec(memory_space=pl.ANY)
     vm = pl.BlockSpec(memory_space=pltpu.VMEM)
-    F, HR = pl.pallas_call(
+    gmax = max(GB) * 128
+    F, HR, handed = pl.pallas_call(
         comm_kernel,
-        out_shape=(jax.ShapeDtypeStruct((4, 4, 4, CAP, 4096), bf), jax.ShapeDtypeStruct((4, 4, 4, CAP, 1024), bf)),
-        in_specs=[any_, any_, vm, vm, vm], out_specs=(any_, any_),
-        scratch_shapes=[V((4, 4, 128, g * 128 + 128), bf) for g in GB]
+        out_shape=(jax.ShapeDtypeStruct((4, 4, 4, CAP, 4096), bf), jax.ShapeDtypeStruct((4, 4, 4, CAP, 1024), bf),
+                   jax.ShapeDtypeStruct((128, 4096), bf)),
+        in_specs=[vm, vm, vm, any_, any_, any_], out_specs=(any_, any_, any_),
+        scratch_shapes=[V((1024, 1024), bf), V((4, 4, 4, CAP, 1024), bf), V((1024, 4096), bf), V((2, 4, 4, CAP, gmax), bf),
+                        V((384, gmax), bf), V((3, 4, 4, 1, 128), f32), V((3, 64, 1, 128), f32), V((128, 4096), bf),
+                        V((64, 128), f32), V((64, 128), f32)]
+        + [V((4, 4, 128, g * 128 + 128), bf) for g in GB]
         + [V((4, 4, 4, CAP, g * 128), bf) for g in GB]
         + [V((3, 4, 4, CAP, h * 128), bf) for h in HB]
         + [V((4, 4, 4, CAP, h * 128), bf) for h in HB]
         + [V((3, 4, 4, CAP, h * 128), bf) for h in HB]
         + [D((3, 2)), D((3, 4)), D((3, 4)), D((3, 4, 4)), D((3, 4, 4)), D((3, 4, 3)), D((3, 4, 3)), D((3, 4)),
-           D((3, 3)), D((3, 3)), D((3, 3)), D((3, 3)), D((3, 4, 3)), D((3, 4, 3)), D((3, 4))],
-        compiler_params=pltpu.CompilerParams(has_side_effects=True, vmem_limit_bytes=62 * 2**20),
-    )(grad, rt, hid, tgt, wgt)
-    return F.reshape(64 * CAP, 4096), HR.reshape(64 * CAP, 1024)
+           D((3, 3)), D((3, 3)), D((3, 3)), D((3, 3)), D((3, 4, 3)), D((3, 4, 3)),
+           D((2,)), D((1,)), D((3,)), D((3,)), D((1,)), D((3,)), D((3,))],
+        compiler_params=pltpu.CompilerParams(has_side_effects=True, vmem_limit_bytes=63 * 2**20),
+    )(routes, scores, router, grad, hidden, down)
+    return F.reshape(64 * CAP, 4096), HR.reshape(64 * CAP, 1024), handed
 
 
 def body(grad_out, saved_hidden, routes, scores, down_weight, router):
-    grad_rows, route_ids, score_rows = grad_out[0], routes[0], scores[0]
-    expert_down, router_rows = down_weight[0, 0], router[0]
     n_tokens, n_routes, hidden_width = saved_hidden.shape[1:]
-    n_experts = router_rows.shape[0]
     hidden_flat = saved_hidden[0].reshape(n_tokens * n_routes, hidden_width)
-    ids = jnp.arange(n_experts, dtype=jnp.int32)
-    onehot = (route_ids[:, :, None] == ids).astype(jnp.float32)
-    member = jnp.sum(onehot, axis=1)
-    t = jnp.arange(n_tokens, dtype=jnp.int32)
-    tril = (t[:, None] > t[None, :]).astype(jnp.bfloat16)
-    rank = jnp.dot(tril, member.astype(jnp.bfloat16), preferred_element_type=jnp.float32)
-    code = jnp.where(member > 0, rank, -1.0)
-    rt = jnp.zeros((128, 128), jnp.bfloat16).at[:n_experts].set(code.T.astype(jnp.bfloat16))
-    slot = jnp.sum(onehot * rank[:, None, :], axis=2).astype(jnp.int32)
-    target = route_ids * CAP + slot
-    total = jnp.sum(score_rows, axis=1, keepdims=True)
-    weights = score_rows / total
-    low = weights.astype(jnp.bfloat16).astype(jnp.float32)
-    grad_recv, hidden_recv = exchange(grad_rows, rt, hidden_flat, target.reshape(1, -1), low.reshape(1, -1))
-    proj = lax.dot_general(grad_recv, expert_down, (((1,), (1,)), ((), ())), preferred_element_type=jnp.float32)
-    derivs = jnp.sum(proj * hidden_recv.astype(jnp.float32), axis=1)
-    back = lax.all_to_all(derivs.reshape(n_experts, CAP), "expert", split_axis=0, concat_axis=0, tiled=True)
+    grad_recv, hidden_recv, handed = exchange(routes[0], scores[0], router[0], grad_out[0], hidden_flat, down_weight[0, 0])
     weight_out = lax.dot_general(hidden_recv, grad_recv, (((0,), (0,)), ((), ())), preferred_element_type=jnp.float32).astype(jnp.bfloat16)
-    home = jnp.zeros((n_tokens, n_experts), jnp.float32)
-    for s in range(CAP):
-        home = home + jnp.where(code == s, back[:, s][None, :], 0.0)
-    rd = jnp.sum(onehot * home[:, None, :], axis=2) / low
-    center = jnp.sum(weights * rd, axis=1, keepdims=True)
-    logit = score_rows * (1.0 - score_rows) / total * (rd - center)
-    dense = jnp.sum(onehot * logit[:, :, None], axis=1)
-    inp = grad_rows.astype(jnp.float32) + jnp.dot(dense, router_rows.astype(jnp.float32))
-    handed = lax.ppermute(inp.astype(jnp.bfloat16), "section", [(0, 1), (1, 0)])
     return weight_out[None, None], handed[None]
 
 

time: 243 us -> 210 us (0.86)
  Pallas kernels: 162 us -> 186 us
  matrix products: 38.9 us -> 19.4 us
  blocking collectives: 17.4 us -> 0 us
  other arithmetic: 9.85 us -> 0 us
  local copies, waits for them, and re-layouts: 10.6 us -> 3.81 us
  starting transfers between devices: 2.48 us -> 0 us
    pallas_call x1, Pallas kernels: 162 us -> 186 us  [exchange(): pl.pallas_call(comm_kernel, out_shape=(jax.ShapeDtypeStruct((4, 4, 4, CAP...]
    dot_general x3 -> x0, matrix products: 19.6 us -> none  [the longest x1 19 us: body(): lax.dot_general(grad_recv, expert_down, (((1,), (1,)), ((), ())), preferr...]
    all_to_all x1 -> x0, blocking collectives: 17.4 us -> none  [body(): lax.all_to_all(derivs.reshape(n_experts, CAP), 'expert', split_axis=0, co...]
    convert_element_type x3 -> x0, local copies, waits for them, and re-layouts: 6.79 us -> none  [the longest x1 6.59 us: body(): derivs = jnp.sum(proj * hidden_recv.astype(jnp.float32), axis=1)]
    convert_element_type x4 -> x0, other arithmetic: 5.95 us -> none  [the longest x1 5.34 us: body(): derivs = jnp.sum(proj * hidden_recv.astype(jnp.float32), axis=1)]
    ppermute x1 -> x0, starting transfers between devices: 2.48 us -> none  [body(): handed = lax.ppermute(inp.astype(jnp.bfloat16), 'section', [(0, 1), (1, 0)])]
  transfers between devices with their start and end apart: 1 -> 0, of which waited for: 0 -> 0; matrix products, arithmetic and copies ran while one was open for 8% -> 0% of each run, Pallas kernels for 0% -> 0%
where the time goes in v2:
time: 210 us
  Pallas kernels  186 us (89%)
  matrix products  19.4 us (9%)
  local copies, waits for them, and re-layouts  3.81 us (2%)
    pallas_call x1, Pallas kernels, exchange(): pl.pallas_call(comm_kernel, out_shape=(jax.ShapeDtypeStruct((4, 4, 4, CAP...  186 us
    dot_general x1, matrix products, body(): lax.dot_general(hidden_recv, grad_recv, (((0,), (0,)), ((), ())), preferr...  19.4 us

profile of v2, /device:TPU:1, one launch (start us, length us, event | category | flops | bytes accessed | tf_op | source)
XLA Modules:
  0.0 209.5 jit_solution(17872272012632163262)
XLA Ops:
  0.6 1.4 copy.8
  2.0 1.4 copy.9
  3.5 185.7 %shard_map.77 = (bf16[4,4,4,24,4096]{4,3,2,1,0:T(8,128)(2,1)}, bf16[4,4,4,24,1024]{4,3,2,1,0:T(8,128)(2,1)}, bf16[128,4096]{1,0:T(8,128)(2,1)}) custom-call(s32[128,8]{1,0:T(8,128)} %bitcast.22, f32[128,8]{1,0:T(8,128)} %bitcast.23, bf16[64,4096]{1,0:T(8,128)(2,1)} %bitcast.21, bf16[128,4096]{1,0:T(8,128)(2,1)} %bitcast.19, bf16[1024,1024]{1,0:T(8,128)(2,1)} %bitcast.18, ...), custom_call_target="tpu_custom_call" | custom-call | tf_op jit(solution)/shard_map/pallas_call | solution.py:347
  189.1 0.0 copy-start
  189.1 19.4 %fusion = bf16[1,1,1024,4096]{3,2,1,0:T(8,128)(2,1)} fusion(bf16[4,4,4,24,1024]{4,3,2,1,0:T(8,128)(2,1)} %get-tuple-element.5, bf16[4,4,4,24,4096]{4,3,2,1,0:T(8,128)(2,1)} %get-tuple-element.6), kind=kOutput, calls=%fused_computation.1 | convolution fusion | flops 12889096192 | bytes 24117248 | tf_op jit(solution)/shard_map/dot_general | solution.py:372
  208.5 0.0 copy-done
  208.5 1.0 copy.12
Async XLA Ops:
  189.1 19.4 %copy-start = (bf16[128,4096]{1,0:T(8,128)(2,1)S(1)}, bf16[128,4096]{1,0:T(8,128)(2,1)}, u32[]{:S(2)}) copy-start(bf16[128,4096]{1,0:T(8,128)(2,1)} %get-tuple-element.7) | copy-start | bytes 3145732

commit v3 on v2

--- a/solution.py
+++ b/solution.py
@@ -37,6 +37,13 @@
     def rcopy(src, dst, ss, rs, axis, delta):
         return pltpu.make_async_remote_copy(src_ref=src, dst_ref=dst, send_sem=ss, recv_sem=rs,
                                             device_id=peer(axis, delta), device_id_type=MESH)
+
+    other = {"section": 1 - lax.axis_index("section")}
+    barrier = pltpu.get_barrier_semaphore()
+    for axis in range(3):
+        for d in (1, 2, 3):
+            pl.semaphore_signal(barrier, inc=1, device_id=peer(axis, d), device_id_type=MESH)
+    pl.semaphore_signal(barrier, inc=1, device_id=other, device_id_type=MESH)
 
     sends = []
 
@@ -58,8 +65,8 @@
     wload.start()
 
     f32, bf = jnp.float32, jnp.bfloat16
-    ri = jnp.transpose(routes[...].astype(f32))
-    st = jnp.transpose(scores[...])
+    ri = routes[...].astype(f32)
+    st = scores[...]
     tot = jnp.sum(st, axis=0, keepdims=True)
     low = (st / tot).astype(bf)
     eio = lax.broadcasted_iota(jnp.int32, (64, 128), 0).astype(f32)
@@ -93,6 +100,7 @@
         acp.append(ring(p, A, lambda d, p=p, A=A, B=B: gb[p].at[co[B], wrap(co[A] + d)], gas, gar, (p,)))
         for k, da in enumerate((0, -1, 1, 2)):
             bcp[p, k] = ring(p, B, lambda d, p=p, A=A, B=B, da=da: gb[p].at[wrap(co[B] + d), wrap(co[A] + da)], gbs, gbr, (p, k))
+    pl.semaphore_wait(barrier, 10)
     for p in range(3):
         loads[p].wait()
         go(acp[p][0]); go(acp[p][1])
@@ -316,7 +324,6 @@
     center = jnp.sum(weight * rd, axis=0, keepdims=True)
     logit = score_e * (1.0 - score_e) / tot * (rd - center)
     lt = jnp.transpose(logit).astype(bf)
-    other = {"section": 1 - lax.axis_index("section")}
     hcps = []
     for p, (A, B, C) in enumerate(ORDERS):
         gw = GB[p] * 128
@@ -360,7 +367,7 @@
         + [D((3, 2)), D((3, 4)), D((3, 4)), D((3, 4, 4)), D((3, 4, 4)), D((3, 4, 3)), D((3, 4, 3)), D((3, 4)),
            D((3, 3)), D((3, 3)), D((3, 3)), D((3, 3)), D((3, 4, 3)), D((3, 4, 3)),
            D((2,)), D((1,)), D((3,)), D((3,)), D((1,)), D((3,)), D((3,))],
-        compiler_params=pltpu.CompilerParams(has_side_effects=True, vmem_limit_bytes=63 * 2**20),
+        compiler_params=pltpu.CompilerParams(has_side_effects=True, collective_id=0, vmem_limit_bytes=63 * 2**20),
     )(routes, scores, router, grad, hidden, down)
     return F.reshape(64 * CAP, 4096), HR.reshape(64 * CAP, 1024), handed
 
@@ -368,7 +375,7 @@
 def body(grad_out, saved_hidden, routes, scores, down_weight, router):
     n_tokens, n_routes, hidden_width = saved_hidden.shape[1:]
     hidden_flat = saved_hidden[0].reshape(n_tokens * n_routes, hidden_width)
-    grad_recv, hidden_recv, handed = exchange(routes[0], scores[0], router[0], grad_out[0], hidden_flat, down_weight[0, 0])
+    grad_recv, hidden_recv, handed = exchange(routes[0].T, scores[0].T, router[0], grad_out[0], hidden_flat, down_weight[0, 0])
     weight_out = lax.dot_general(hidden_recv, grad_recv, (((0,), (0,)), ((), ())), preferred_element_type=jnp.float32).astype(jnp.bfloat16)
     return weight_out[None, None], handed[None]
 

time: 210 us -> 199 us (0.948)
  Pallas kernels: 186 us -> 178 us
  local copies, waits for them, and re-layouts: 3.81 us -> 0.97 us
    pallas_call x1, Pallas kernels: 186 us -> 178 us  [exchange(): pl.pallas_call(comm_kernel, out_shape=(jax.ShapeDtypeStruct((4, 4, 4, CAP...]
    unnamed x5 -> x3, local copies, waits for them, and re-layouts: 3.81 us -> 0.97 us
where the time goes in v3:
time: 199 us
  Pallas kernels  178 us (89%)
  matrix products  19.4 us (10%)
    pallas_call x1, Pallas kernels, exchange(): pl.pallas_call(comm_kernel, out_shape=(jax.ShapeDtypeStruct((4, 4, 4, CAP...  178 us
    dot_general x1, matrix products, body(): lax.dot_general(hidden_recv, grad_recv, (((0,), (0,)), ((), ())), preferr...  19.4 us

profile of v3, /device:TPU:1, one launch (start us, length us, event | category | flops | bytes accessed | tf_op | source)
XLA Modules:
  0.0 198.8 jit_solution(501040826876972354)
XLA Ops:
  0.6 177.8 %shard_map.77 = (bf16[4,4,4,24,4096]{4,3,2,1,0:T(8,128)(2,1)}, bf16[4,4,4,24,1024]{4,3,2,1,0:T(8,128)(2,1)}, bf16[128,4096]{1,0:T(8,128)(2,1)}) custom-call(s32[8,128]{1,0:T(8,128)} %bitcast.26, f32[8,128]{1,0:T(8,128)} %bitcast.27, bf16[64,4096]{1,0:T(8,128)(2,1)} %bitcast.25, bf16[128,4096]{1,0:T(8,128)(2,1)} %bitcast.23, bf16[1024,1024]{1,0:T(8,128)(2,1)} %bitcast.22, ...), custom_call_target="tpu_custom_call" | custom-call | tf_op jit(solution)/shard_map/pallas_call | solution.py:354
  178.5 0.0 copy-start
  178.5 19.4 %fusion = bf16[1,1,1024,4096]{3,2,1,0:T(8,128)(2,1)} fusion(bf16[4,4,4,24,1024]{4,3,2,1,0:T(8,128)(2,1)} %get-tuple-element.5, bf16[4,4,4,24,4096]{4,3,2,1,0:T(8,128)(2,1)} %get-tuple-element.6), kind=kOutput, calls=%fused_computation.1 | convolution fusion | flops 12889096192 | bytes 24117248 | tf_op jit(solution)/shard_map/dot_general | solution.py:379
  197.9 0.0 copy-done
  197.9 1.0 copy.10
Async XLA Ops:
  178.5 19.4 %copy-start = (bf16[128,4096]{1,0:T(8,128)(2,1)S(1)}, bf16[128,4096]{1,0:T(8,128)(2,1)}, u32[]{:S(2)}) copy-start(bf16[128,4096]{1,0:T(8,128)(2,1)} %get-tuple-element.7) | copy-start | bytes 3145732

commit v4 on v3

--- a/solution.py
+++ b/solution.py
@@ -10,6 +10,7 @@
 CAP = 24
 ORDERS = ((0, 1, 2), (1, 2, 0), (2, 0, 1))
 STRIDE = (16, 4, 1)
+CHUNK = {0: 0, -1: 1, 1: 2, 2: 3}
 GB = (10, 12, 10)
 HB = (2, 3, 3)
 
@@ -18,13 +19,14 @@
     return tuple(128 * sum(blocks[:i]) for i in range(len(blocks)))
 
 
-def comm_kernel(routes, scores, router, grad, hidden, down, F, HR, handed, hid, HV, wv, gch, g2, ds, dr, hnd, codes_s, score_s,
+def comm_kernel(routes, scores, router, grad, hidden, down, F, HT, part, handed, hid, HV, wv, gch, g2, acc_s, stage, U0, U1, U2, lv0, lv1, lv2, ds, dr, hnd, codes_s, score_s,
                 gb0, gb1, gb2, sc0, sc1, sc2, ha0, ha1, ha2, hb0, hb1, hb2, hc0, hc1, hc2,
-                lsem, gas, gar, gbs, gbr, gcs, gcr, gcl, has, har, hbs, hbr, hcs, hcr, gls, wsem, dss, drs, hos, hns, hnr):
+                lsem, gas, gar, gbs, gbr, gcs, gcr, gcl, has, har, hbs, hbr, hcs, hcr, gls, wsem, dss, drs, hos, pos, lvs, hns, hnr):
     gb, sc, ha, hb, hc = (gb0, gb1, gb2), (sc0, sc1, sc2), (ha0, ha1, ha2), (hb0, hb1, hb2), (hc0, hc1, hc2)
     e = lax.axis_index("expert")
     co = (e // 16, (e // 4) % 4, e % 4)
     gcol, hcol = starts(GB), starts(HB)
+    U, lv = (U0, U1, U2), (lv0, lv1, lv2)
 
     def wrap(v):
         return lax.rem(v + 4, 4)
@@ -172,22 +174,38 @@
             rows = jnp.dot(sel, gb[p][bb, a, :, 0:gw], preferred_element_type=jnp.float32)
             rows = rows.reshape(4, CAP, gw).astype(jnp.bfloat16)
             for dc in range(4):
-                sc[p][dc, db % 4, a] = rows[dc]
+                if db == 2 and dc == 0:
+                    if A < C:
+                        lv[p][a, co[C]] = rows[0]
+                    else:
+                        lv[p][co[C], a] = rows[0]
+                else:
+                    sc[p][dc, n % 3, a] = rows[dc]
             return carry
+        n = CHUNK[db]
+        if db == 2:
+            for cp in csends[p]:
+                cp.wait_send()
+            locals_[p, 0].wait()
         lax.fori_loop(0, 4, one, 0)
         for dc in (1, 3, 2):
-            go(rcopy(sc[p].at[dc, db % 4], fdst(p, bb, 0), gcs.at[p, db % 4, dc - 1], gcr.at[p, db % 4, dc - 1], C, dc))
-        cp = pltpu.make_async_copy(sc[p].at[0, db % 4], fdst(p, bb, 0), gcl.at[p, db % 4])
-        cp.start()
-        locals_[p, db % 4] = cp
-
-    def fdst(p, bb, d):
+            cp = rcopy(sc[p].at[dc, n % 3], fdst(p, db, 0), gcs.at[p, n, dc - 1], gcr.at[p, n, dc - 1], C, dc)
+            cp.start()
+            (csends[p] if db == 0 else sends).append(cp)
+        if db != 2:
+            cp = pltpu.make_async_copy(sc[p].at[0, n % 3], fdst(p, db, 0), gcl.at[p, n])
+            cp.start()
+            locals_[p, n] = cp
+
+    csends = ([], [], [])
+
+    def fdst(p, db, d):
         A, B, C = ORDERS[p]
-        idx = [None, None, None]
-        idx[A] = slice(None)
-        idx[B] = bb
-        idx[C] = wrap(co[C] - d)
-        return F.at[idx[0], idx[1], idx[2], :, pl.ds(gcol[p], GB[p] * 128)]
+        c = wrap(co[C] - d)
+        if db == 2:
+            return lv[p].at[:, c] if A < C else lv[p].at[c, :]
+        cols = pl.ds(gcol[p], GB[p] * 128)
+        return F.at[CHUNK[db], :, c, :, cols] if A < C else F.at[CHUNK[db], c, :, :, cols]
 
     def hdst(p, bb, d):
         A, B, C = ORDERS[p]
@@ -242,47 +260,84 @@
             for dc in (1, 3, 2):
                 src = hc[p].at[max(d - 1, 0), :, 0]
                 rcopy(src, hdst(p, wrap(co[B] - d), dc), hcs.at[p, d, dc - 1], hcr.at[p, d, dc - 1], C, dc).wait_recv()
-    hout = pltpu.make_async_copy(HV, HR, hos.at[0])
-    hout.start()
     wload.wait()
 
     def rest(p):
         return tuple(ax for ax in range(3) if ax != ORDERS[p][1])
 
-    def at_b(ref, p, bb):
+    def hview(p, db):
         idx = [slice(None)] * 3
-        idx[ORDERS[p][1]] = bb
-        return ref.at[idx[0], idx[1], idx[2]]
-
-    chunks = [(p, db) for db in (0, -1, 1, 2) for p in range(3)]
-
-    def load(n):
-        p, db = chunks[n]
-        C = ORDERS[p][2]
-        bb = wrap(co[ORDERS[p][1]] + db)
+        idx[ORDERS[p][1]] = wrap(co[ORDERS[p][1]] + db)
+        return HV.at[idx[0], idx[1], idx[2]]
+
+    def turn(p, db, off):
+        view = hview(p, db)
+
+        def one(j, carry):
+            v = view[:, :, :, pl.ds(pl.multiple_of(j * 128, 128), 128)].astype(f32).reshape(384, 128)
+            hid[pl.ds(pl.multiple_of(j * 128, 128), 128), off:off + 384] = jnp.transpose(v).astype(bf)
+            return carry
+        lax.fori_loop(0, 8, one, 0)
+
+    for p in range(3):
+        gw = GB[p] * 128
+        turn(p, 1, 0)
+        turn(p, 2, 384)
+        cp = pltpu.make_async_copy(hid.at[:, pl.ds(0, 768)], HT.at[p], hos.at[0])
+        cp.start()
+        view = hview(p, 2)
+        for i in range(4):
+            g2[i * 96:(i + 1) * 96, 0:1024] = view[i].astype(f32).reshape(96, 1024).astype(bf)
+
+        def prod(ct, carry, p=p):
+            cols = pl.ds(pl.multiple_of(ct * 256, 256), 256)
+            wcols = pl.ds(pl.multiple_of(gcol[p] + ct * 256, 256), 256)
+            u = jnp.dot(g2[0:384, 0:1024], wv[:, wcols], preferred_element_type=f32)
+            U[p][:, :, :, cols] = u.reshape(4, 4, CAP, 256).astype(bf)
+            return carry
+        lax.fori_loop(0, gw // 256, prod, 0)
+        cp.wait()
+
+    def arrived(p, db):
+        C, n = ORDERS[p][2], CHUNK[db]
         for dc in (1, 3, 2):
-            rcopy(sc[p].at[dc, db % 4], fdst(p, bb, dc), gcs.at[p, db % 4, dc - 1], gcr.at[p, db % 4, dc - 1], C, dc).wait_recv()
-        locals_[p, db % 4].wait()
-        gw = GB[p] * 128
-        cp = pltpu.make_async_copy(at_b(F, p, bb).at[:, :, :, pl.ds(gcol[p], gw)], gch.at[n % 2, :, :, :, pl.ds(0, gw)], gls.at[n % 2])
+            rcopy(sc[p].at[dc, n % 3], fdst(p, db, dc), gcs.at[p, n, dc - 1], gcr.at[p, n, dc - 1], C, dc).wait_recv()
+        if n in (1, 2):
+            locals_[p, n].wait()
+
+    def load(p, db, slot):
+        gw = GB[p] * 128
+        arrived(p, db)
+        cp = pltpu.make_async_copy(F.at[CHUNK[db], :, :, :, pl.ds(gcol[p], gw)], gch.at[slot, :, :, :, pl.ds(0, gw)], gls.at[slot])
         cp.start()
         return cp
 
-    def derive(n):
-        p, db = chunks[n]
-        gw = GB[p] * 128
+    def relay(p, slot, r0):
+        gw = GB[p] * 128
+        for i in range(4):
+            g2[r0 + i * 96:r0 + (i + 1) * 96, 0:gw] = gch[slot, i, :, :, 0:gw].astype(f32).reshape(96, gw).astype(bf)
+
+    def derive(p, dbs):
+        gw = GB[p] * 128
+        m = 384 * len(dbs)
+
+        def one(f, carry):
+            rows = pl.ds(pl.multiple_of(f * 256, 256), 256)
+            proj = lax.dot_general(g2[0:m, 0:gw], wv[rows, gcol[p]:gcol[p] + gw], (((1,), (1,)), ((), ())),
+                                   preferred_element_type=f32)
+            for k, db in enumerate(dbs):
+                h = hview(p, db)[:, :, :, rows].astype(f32).reshape(384, 256)
+                q = proj[k * 384:(k + 1) * 384] * h
+                acc_s[k * 384:(k + 1) * 384, :] = jnp.where(f > 0, acc_s[k * 384:(k + 1) * 384, :], 0.0) + q[:, 0:128] + q[:, 128:256]
+            return carry
+        lax.fori_loop(0, 4, one, 0)
+        for k, db in enumerate(dbs):
+            give(p, db, acc_s[k * 384:(k + 1) * 384, :])
+
+    def give(p, db, acc):
         B = ORDERS[p][1]
         bb = wrap(co[B] + db)
         R1, R2 = rest(p)
-        for i in range(4):
-            g2[i * 96:(i + 1) * 96, 0:gw] = gch[n % 2, i, :, :, 0:gw].astype(f32).reshape(96, gw).astype(bf)
-        hview = at_b(HV, p, bb)
-        acc = jnp.zeros((384, 128), f32)
-        for f in range(4):
-            proj = lax.dot_general(g2[:, 0:gw], wv[f * 256:(f + 1) * 256, gcol[p]:gcol[p] + gw], (((1,), (1,)), ((), ())),
-                                   preferred_element_type=f32)
-            q = proj * hview[:, :, :, f * 256:(f + 1) * 256].astype(f32).reshape(384, 256)
-            acc = acc + q[:, 0:128] + q[:, 128:256]
         pad = jnp.concatenate([acc.reshape(16, CAP, 128), jnp.zeros((16, 8, 128), f32)], axis=1).reshape(512, 128)
         row = jnp.sum(jnp.transpose(pad), axis=0, keepdims=True)
         for i in range(4):
@@ -298,12 +353,60 @@
                 pltpu.make_async_remote_copy(src_ref=ds.at[p, db % 4, i], dst_ref=dr.at[p, e], send_sem=dss.at[p], recv_sem=drs.at[p],
                                              device_id={"expert": c[0] * 16 + c[1] * 4 + c[2]}, device_id_type=MESH).start()
 
-    cur = load(0)
-    for n in range(12):
-        nxt = load(n + 1) if n < 11 else None
-        cur.wait()
-        derive(n)
-        cur = nxt
+    def gradient(p):
+        gw = GB[p] * 128
+
+        def out(ct, slot):
+            cols = pl.ds(pl.multiple_of(gcol[p] + ct * 256, 256), 256)
+            return pltpu.make_async_copy(stage.at[slot], part.at[:, cols], pos.at[slot])
+
+        def one(ct, carry):
+            slot = lax.rem(ct, 2)
+
+            @pl.when(ct >= 2)
+            def _():
+                out(ct - 2, slot).wait()
+            stage[slot] = jnp.dot(hid[:, 0:768], g2[:, pl.ds(pl.multiple_of(ct * 256, 256), 256)], preferred_element_type=f32).astype(bf)
+            out(ct, slot).start()
+            return carry
+        n = gw // 256
+        lax.fori_loop(0, n, one, 0)
+        out(n - 2, (n - 2) % 2).wait()
+        out(n - 1, (n - 1) % 2).wait()
+
+    cur = (load(0, 0, 0), load(0, -1, 1))
+    for p in range(3):
+        turn(p, 0, 0)
+        turn(p, -1, 384)
+        cur[0].wait(); relay(p, 0, 0)
+        cur[1].wait(); relay(p, 1, 384)
+        if p < 2:
+            cur = (load(p + 1, 0, 0), load(p + 1, -1, 1))
+        derive(p, (0, -1))
+        gradient(p)
+    cur = load(0, 1, 0)
+    for p in range(3):
+        cur.wait(); relay(p, p % 2, 0)
+        if p < 2:
+            cur = load(p + 1, 1, (p + 1) % 2)
+        derive(p, (1,))
+    lcps = []
+    for p in range(3):
+        gw = GB[p] * 128
+        arrived(p, 2)
+        cp = pltpu.make_async_copy(lv[p], F.at[3, :, :, :, pl.ds(gcol[p], gw)], lvs.at[p])
+        cp.start()
+        lcps.append(cp)
+
+        def one(ij, carry, p=p):
+            i, j = ij // 4, lax.rem(ij, 4)
+            t = jnp.zeros((CAP, 128), f32)
+            for k in range(GB[p]):
+                t = t + U[p][i, j, :, k * 128:(k + 1) * 128].astype(f32) * lv[p][i, j, :, k * 128:(k + 1) * 128].astype(f32)
+            acc_s[pl.ds(pl.multiple_of(ij * CAP, 8), CAP), :] = t
+            return carry
+        lax.fori_loop(0, 16, one, 0)
+        give(p, 2, acc_s[0:384, :])
 
     home = jnp.zeros((64, 128), f32)
     window = lax.broadcasted_iota(jnp.int32, (64, 128), 1) // 32
@@ -337,7 +440,8 @@
         hcps.append(cp)
     for p in range(3):
         pltpu.make_async_copy(dr.at[p, pl.ds(0, 63)], dr.at[p, pl.ds(0, 63)], dss.at[p]).wait()
-    hout.wait()
+    for cp in lcps:
+        cp.wait()
     for cp in sends:
         cp.wait_send()
     for cp in hcps:
@@ -351,32 +455,53 @@
     any_ = pl.BlockSpec(memory_space=pl.ANY)
     vm = pl.BlockSpec(memory_space=pltpu.VMEM)
     gmax = max(GB) * 128
-    F, HR, handed = pl.pallas_call(
+    F, HT, part, handed = pl.pallas_call(
         comm_kernel,
-        out_shape=(jax.ShapeDtypeStruct((4, 4, 4, CAP, 4096), bf), jax.ShapeDtypeStruct((4, 4, 4, CAP, 1024), bf),
-                   jax.ShapeDtypeStruct((128, 4096), bf)),
-        in_specs=[vm, vm, vm, any_, any_, any_], out_specs=(any_, any_, any_),
+        out_shape=(jax.ShapeDtypeStruct((4, 4, 4, CAP, 4096), bf), jax.ShapeDtypeStruct((3, 1024, 768), bf),
+                   jax.ShapeDtypeStruct((1024, 4096), bf), jax.ShapeDtypeStruct((128, 4096), bf)),
+        in_specs=[vm, vm, vm, any_, any_, any_], out_specs=(any_, any_, any_, any_),
         scratch_shapes=[V((1024, 1024), bf), V((4, 4, 4, CAP, 1024), bf), V((1024, 4096), bf), V((2, 4, 4, CAP, gmax), bf),
-                        V((384, gmax), bf), V((3, 4, 4, 1, 128), f32), V((3, 64, 1, 128), f32), V((128, 4096), bf),
+                        V((768, gmax), bf), V((768, 128), f32), V((2, 1024, 256), bf)]
+        + [V((4, 4, CAP, g * 128), bf) for g in GB] * 2
+        + [V((3, 4, 4, 1, 128), f32), V((3, 64, 1, 128), f32), V((128, 4096), bf),
                         V((64, 128), f32), V((64, 128), f32)]
         + [V((4, 4, 128, g * 128 + 128), bf) for g in GB]
-        + [V((4, 4, 4, CAP, g * 128), bf) for g in GB]
+        + [V((4, 3, 4, CAP, g * 128), bf) for g in GB]
         + [V((3, 4, 4, CAP, h * 128), bf) for h in HB]
         + [V((4, 4, 4, CAP, h * 128), bf) for h in HB]
         + [V((3, 4, 4, CAP, h * 128), bf) for h in HB]
         + [D((3, 2)), D((3, 4)), D((3, 4)), D((3, 4, 4)), D((3, 4, 4)), D((3, 4, 3)), D((3, 4, 3)), D((3, 4)),
            D((3, 3)), D((3, 3)), D((3, 3)), D((3, 3)), D((3, 4, 3)), D((3, 4, 3)),
-           D((2,)), D((1,)), D((3,)), D((3,)), D((1,)), D((3,)), D((3,))],
-        compiler_params=pltpu.CompilerParams(has_side_effects=True, collective_id=0, vmem_limit_bytes=63 * 2**20),
+           D((2,)), D((1,)), D((3,)), D((3,)), D((1,)), D((2,)), D((3,)), D((3,)), D((3,))],
+        compiler_params=pltpu.CompilerParams(has_side_effects=True, collective_id=0, vmem_limit_bytes=67043328),
     )(routes, scores, router, grad, hidden, down)
-    return F.reshape(64 * CAP, 4096), HR.reshape(64 * CAP, 1024), handed
+    return F.reshape(64 * CAP, 4096), HT, part, handed
+
+
+def finish_kernel(part, turned, rows, out):
+    more = jnp.dot(turned[0], rows[...], preferred_element_type=jnp.float32)
+    out[...] = (part[...].astype(jnp.float32) + more).astype(jnp.bfloat16)
+
+
+def finish(rows, turned, part):
+    edges = [sum(GB[:i]) // 2 for i in (1, 2)]
+    return pl.pallas_call(
+        finish_kernel,
+        out_shape=jax.ShapeDtypeStruct((1024, 4096), jnp.bfloat16),
+        grid=(16,),
+        in_specs=[pl.BlockSpec((1024, 256), lambda i: (0, i)),
+                  pl.BlockSpec((1, 1024, 768), lambda i: ((i >= edges[0]).astype(jnp.int32) + (i >= edges[1]).astype(jnp.int32), 0, 0)),
+                  pl.BlockSpec((768, 256), lambda i: (1, i))],
+        out_specs=pl.BlockSpec((1024, 256), lambda i: (0, i)),
+        compiler_params=pltpu.CompilerParams(dimension_semantics=("arbitrary",), vmem_limit_bytes=40 * 2**20),
+    )(part, turned, rows)
 
 
 def body(grad_out, saved_hidden, routes, scores, down_weight, router):
     n_tokens, n_routes, hidden_width = saved_hidden.shape[1:]
     hidden_flat = saved_hidden[0].reshape(n_tokens * n_routes, hidden_width)
-    grad_recv, hidden_recv, handed = exchange(routes[0].T, scores[0].T, router[0], grad_out[0], hidden_flat, down_weight[0, 0])
-    weight_out = lax.dot_general(hidden_recv, grad_recv, (((0,), (0,)), ((), ())), preferred_element_type=jnp.float32).astype(jnp.bfloat16)
+    rows, turned, part, handed = exchange(routes[0].T, scores[0].T, router[0], grad_out[0], hidden_flat, down_weight[0, 0])
+    weight_out = finish(rows, turned, part)
     return weight_out[None, None], handed[None]
 
 

time: 199 us -> 233 us (1.17)
  Pallas kernels: 178 us -> 225 us
  matrix products: 19.4 us -> 0 us
  local copies, waits for them, and re-layouts: 0.97 us -> 6.68 us
    pallas_call x1, Pallas kernels: 178 us -> 209 us  [exchange(): pl.pallas_call(comm_kernel, out_shape=(jax.ShapeDtypeStruct((4, 4, 4, CAP...]
    dot_general x1 -> x0, matrix products: 19.4 us -> none  [body(): lax.dot_general(hidden_recv, grad_recv, (((0,), (0,)), ((), ())), preferr...]
    pallas_call x0 -> x1, Pallas kernels: none -> 15.8 us  [finish(): pl.pallas_call(finish_kernel, out_shape=jax.ShapeDtypeStruct((1024, 4096)...]
    unnamed x3 -> x7, local copies, waits for them, and re-layouts: 0.97 us -> 6.68 us
where the time goes in v4:
time: 233 us; the launch traced here: 232 us
  Pallas kernels  225 us (97%)
  local copies, waits for them, and re-layouts  6.68 us (3%)
    pallas_call x1, Pallas kernels, exchange(): pl.pallas_call(comm_kernel, out_shape=(jax.ShapeDtypeStruct((4, 4, 4, CAP...  209 us
    pallas_call x1, Pallas kernels, finish(): pl.pallas_call(finish_kernel, out_shape=jax.ShapeDtypeStruct((1024, 4096)...  15.8 us
    unnamed x7, local copies, waits for them, and re-layouts  6.68 us

profile of v4, /device:TPU:1, one launch (start us, length us, event | category | flops | bytes accessed | tf_op | source)
XLA Modules:
  0.0 232.3 jit_solution(13305570451019611608)
XLA Ops:
  0.6 209.2 %shard_map.77 = (bf16[4,4,4,24,4096]{4,3,2,1,0:T(8,128)(2,1)}, bf16[3,1024,768]{2,1,0:T(8,128)(2,1)}, bf16[1024,4096]{1,0:T(8,128)(2,1)}, bf16[128,4096]{1,0:T(8,128)(2,1)}) custom-call(s32[8,128]{1,0:T(8,128)} %bitcast.20, f32[8,128]{1,0:T(8,128)} %bitcast.21, bf16[64,4096]{1,0:T(8,128)(2,1)} %bitcast.19, bf16[128,4096]{1,0:T(8,128)(2,1)} %bitcast.17, ...), custom_call_target="tpu_custom_call" | custom-call | tf_op jit(solution)/shard_map/pallas_call | solution.py:458
  209.8 0.0 copy-start
  209.8 3.4 %copy-done = bf16[1024,4096]{1,0:T(8,128)(2,1)S(1)} copy-done((bf16[1024,4096]{1,0:T(8,128)(2,1)S(1)}, bf16[1024,4096]{1,0:T(8,128)(2,1)}, u32[]{:S(2)}) %copy-start) | copy-done | bytes 8388632
  213.2 0.0 copy-start.1
  213.2 2.3 %copy-done.1 = bf16[3,1024,768]{2,1,0:T(8,128)(2,1)S(1)} copy-done((bf16[3,1024,768]{2,1,0:T(8,128)(2,1)S(1)}, bf16[3,1024,768]{2,1,0:T(8,128)(2,1)}, u32[]{:S(2)}) %copy-start.1) | copy-done | bytes 4718616
  215.6 0.0 copy-start.2
  215.6 15.8 %shard_map.78 = bf16[1024,4096]{1,0:T(8,128)(2,1)} custom-call(bf16[1024,4096]{1,0:T(8,128)(2,1)S(1)} %copy-done, bf16[3,1024,768]{2,1,0:T(8,128)(2,1)S(1)} %copy-done.1, bf16[1536,4096]{1,0:T(8,128)(2,1)} %bitcast.13), custom_call_target="tpu_custom_call" | custom-call | tf_op jit(solution)/shard_map/pallas_call | solution.py:488
  231.3 0.0 copy-done.2
  231.4 1.0 copy.9
Async XLA Ops:
  209.8 3.4 %copy-start = (bf16[1024,4096]{1,0:T(8,128)(2,1)S(1)}, bf16[1024,4096]{1,0:T(8,128)(2,1)}, u32[]{:S(2)}) copy-start(bf16[1024,4096]{1,0:T(8,128)(2,1)} %get-tuple-element.6.part) | copy-start | bytes 25165828
  213.2 2.3 %copy-start.1 = (bf16[3,1024,768]{2,1,0:T(8,128)(2,1)S(1)}, bf16[3,1024,768]{2,1,0:T(8,128)(2,1)}, u32[]{:S(2)}) copy-start(bf16[3,1024,768]{2,1,0:T(8,128)(2,1)} %get-tuple-element.7.turned) | copy-start | bytes 14155780
  215.6 15.8 %copy-start.2 = (bf16[128,4096]{1,0:T(8,128)(2,1)S(1)}, bf16[128,4096]{1,0:T(8,128)(2,1)}, u32[]{:S(2)}) copy-start(bf16[128,4096]{1,0:T(8,128)(2,1)} %get-tuple-element.9) | copy-start | bytes 3145732

commit v5 on v3

--- a/solution.py
+++ b/solution.py
@@ -18,13 +18,14 @@
     return tuple(128 * sum(blocks[:i]) for i in range(len(blocks)))
 
 
-def comm_kernel(routes, scores, router, grad, hidden, down, F, HR, handed, hid, HV, wv, gch, g2, ds, dr, hnd, codes_s, score_s,
+def comm_kernel(routes, scores, router, grad, hidden, down, F, HR, handed, hid, HV, wv, gch, g2, ds, dr, hnd, codes_s, score_s, tab, rc, U0, U1, U2, lv0, lv1, lv2,
                 gb0, gb1, gb2, sc0, sc1, sc2, ha0, ha1, ha2, hb0, hb1, hb2, hc0, hc1, hc2,
-                lsem, gas, gar, gbs, gbr, gcs, gcr, gcl, has, har, hbs, hbr, hcs, hcr, gls, wsem, dss, drs, hos, hns, hnr):
+                lsem, gas, gar, gbs, gbr, gcs, gcr, gcl, has, har, hbs, hbr, hcs, hcr, gls, wsem, dss, drs, hos, lvs, tss, trs):
     gb, sc, ha, hb, hc = (gb0, gb1, gb2), (sc0, sc1, sc2), (ha0, ha1, ha2), (hb0, hb1, hb2), (hc0, hc1, hc2)
     e = lax.axis_index("expert")
     co = (e // 16, (e // 4) % 4, e % 4)
     gcol, hcol = starts(GB), starts(HB)
+    U, lv = (U0, U1, U2), (lv0, lv1, lv2)
 
     def wrap(v):
         return lax.rem(v + 4, 4)
@@ -38,12 +39,20 @@
         return pltpu.make_async_remote_copy(src_ref=src, dst_ref=dst, send_sem=ss, recv_sem=rs,
                                             device_id=peer(axis, delta), device_id_type=MESH)
 
-    other = {"section": 1 - lax.axis_index("section")}
+    def plane(p, da, db):
+        A, B, C = ORDERS[p]
+        c = list(co)
+        c[A], c[B] = wrap(co[A] + da), wrap(co[B] + db)
+        return c, {"expert": c[0] * 16 + c[1] * 4 + c[2]}
+
     barrier = pltpu.get_barrier_semaphore()
     for axis in range(3):
         for d in (1, 2, 3):
             pl.semaphore_signal(barrier, inc=1, device_id=peer(axis, d), device_id_type=MESH)
-    pl.semaphore_signal(barrier, inc=1, device_id=other, device_id_type=MESH)
+    for p in range(3):
+        for da in (1, 2, 3):
+            for db in (1, 2, 3):
+                pl.semaphore_signal(barrier, inc=1, device_id=plane(p, da, db)[1], device_id_type=MESH)
 
     sends = []
 
@@ -63,6 +72,28 @@
     hload.start()
     wload = pltpu.make_async_copy(down, wv, wsem.at[0])
     wload.start()
+
+    def ring(p, axis, slot_of, sems, semr, idx):
+        gw = GB[p] * 128
+        half = (gw // 256) * 128
+        def cp(i, src_delta, cols, delta):
+            ref = slot_of(src_delta)
+            if cols is not None:
+                ref = ref.at[:, pl.ds(*cols)]
+            return rcopy(ref, ref, sems.at[idx + (i,)], semr.at[idx + (i,)], axis, delta)
+        return (cp(0, 0, None, 1), cp(1, 0, None, -1), cp(2, -1, (0, half), 1), cp(3, 1, (half, gw - half), -1))
+
+    acp, bcp = [], {}
+    for p, (A, B, C) in enumerate(ORDERS):
+        acp.append(ring(p, A, lambda d, p=p, A=A, B=B: gb[p].at[co[B], wrap(co[A] + d)], gas, gar, (p,)))
+        for k, da in enumerate((0, -1, 1, 2)):
+            bcp[p, k] = ring(p, B, lambda d, p=p, A=A, B=B, da=da: gb[p].at[wrap(co[B] + d), wrap(co[A] + da)], gbs, gbr, (p, k))
+    pl.semaphore_wait(barrier, 36)
+    for p in range(3):
+        loads[p].wait()
+        go(acp[p][0]); go(acp[p][1])
+    for p in range(3):
+        go(bcp[p, 0][0]); go(bcp[p, 0][1])
 
     f32, bf = jnp.float32, jnp.bfloat16
     ri = routes[...].astype(f32)
@@ -81,31 +112,22 @@
     code_e = jnp.where(member > 0.0, rank, -1.0)
     codes_s[...] = code_e
     score_s[...] = score_e
-    code_b = jnp.concatenate([code_e, jnp.full((64, 128), -1.0, f32)], axis=0).astype(bf)
-    for p, (A, B, C) in enumerate(ORDERS):
-        gb[p][co[B], co[A], :, GB[p] * 128:GB[p] * 128 + 128] = code_b
-
-    def ring(p, axis, slot_of, sems, semr, idx):
-        gw = GB[p] * 128 + 128
-        half = (gw // 256) * 128
-        def cp(i, src_delta, cols, delta):
-            ref = slot_of(src_delta)
-            if cols is not None:
-                ref = ref.at[:, pl.ds(*cols)]
-            return rcopy(ref, ref, sems.at[idx + (i,)], semr.at[idx + (i,)], axis, delta)
-        return (cp(0, 0, None, 1), cp(1, 0, None, -1), cp(2, -1, (0, half), 1), cp(3, 1, (half, gw - half), -1))
-
-    acp, bcp = [], {}
-    for p, (A, B, C) in enumerate(ORDERS):
-        acp.append(ring(p, A, lambda d, p=p, A=A, B=B: gb[p].at[co[B], wrap(co[A] + d)], gas, gar, (p,)))
-        for k, da in enumerate((0, -1, 1, 2)):
-            bcp[p, k] = ring(p, B, lambda d, p=p, A=A, B=B, da=da: gb[p].at[wrap(co[B] + d), wrap(co[A] + da)], gbs, gbr, (p, k))
-    pl.semaphore_wait(barrier, 10)
-    for p in range(3):
-        loads[p].wait()
-        go(acp[p][0]); go(acp[p][1])
-    for p in range(3):
-        go(bcp[p, 0][0]); go(bcp[p, 0][1])
+    for k in range(64):
+        tab[k // 16, (k // 4) % 4, k % 4] = code_e[k:k + 1, :]
+
+    for p, (A, B, C) in enumerate(ORDERS):
+        for da in range(4):
+            for db in range(4):
+                c, dev = plane(p, da, db)
+                idx = list(c)
+                if da == 0 and db == 0:
+                    for k in range(4):
+                        idx[C] = k
+                        rc[p, co[B] * 4 + co[A], k] = tab[idx[0], idx[1], idx[2]]
+                    continue
+                idx[C] = slice(None)
+                pltpu.make_async_remote_copy(src_ref=tab.at[idx[0], idx[1], idx[2]], dst_ref=rc.at[p, co[B] * 4 + co[A]],
+                                             send_sem=tss.at[p], recv_sem=trs.at[p], device_id=dev, device_id_type=MESH).start()
 
     slots = jnp.concatenate([jnp.sum(jnp.where(eio == ri[k:k + 1, :], rank, 0.0), axis=0, keepdims=True) for k in range(8)], axis=0)
     n8 = lax.broadcasted_iota(jnp.int32, (128, 1024), 1) // 8
@@ -155,37 +177,42 @@
     j = lax.broadcasted_iota(jnp.int32, (4 * CAP, 1), 0)
     dCj = (j >= CAP).astype(jnp.int32) + (j >= 2 * CAP).astype(jnp.int32) + (j >= 3 * CAP).astype(jnp.int32)
     slotj = (j - dCj * CAP).astype(jnp.float32)
-    lane = lax.broadcasted_iota(jnp.int32, (4 * CAP, 64), 1)
 
     def pack(p, db):
         A, B, C = ORDERS[p]
         gw = GB[p] * 128
-        cc = co[C] + dCj
-        cc = jnp.where(cc >= 4, cc - 4, cc)
-        eid = STRIDE[A] * co[A] + STRIDE[B] * co[B] + STRIDE[C] * cc
-        E = jnp.where(lane == eid, 1.0, 0.0).astype(jnp.bfloat16)
         bb = wrap(co[B] + db)
 
         def one(a, carry):
-            codes = jnp.dot(E, gb[p][bb, a, 0:64, gw:gw + 128], preferred_element_type=jnp.float32)
+            codes = jnp.concatenate([jnp.broadcast_to(rc[p, bb * 4 + a, wrap(co[C] + dc)], (CAP, 128)) for dc in range(4)], axis=0)
             sel = jnp.where(codes == slotj, 1.0, 0.0).astype(jnp.bfloat16)
             rows = jnp.dot(sel, gb[p][bb, a, :, 0:gw], preferred_element_type=jnp.float32)
             rows = rows.reshape(4, CAP, gw).astype(jnp.bfloat16)
             for dc in range(4):
-                sc[p][dc, db % 4, a] = rows[dc]
+                if db == 2 and dc == 0:
+                    if A < C:
+                        lv[p][a, co[C]] = rows[0]
+                    else:
+                        lv[p][co[C], a] = rows[0]
+                else:
+                    sc[p][dc, db % 4, a] = rows[dc]
             return carry
         lax.fori_loop(0, 4, one, 0)
         for dc in (1, 3, 2):
-            go(rcopy(sc[p].at[dc, db % 4], fdst(p, bb, 0), gcs.at[p, db % 4, dc - 1], gcr.at[p, db % 4, dc - 1], C, dc))
-        cp = pltpu.make_async_copy(sc[p].at[0, db % 4], fdst(p, bb, 0), gcl.at[p, db % 4])
-        cp.start()
-        locals_[p, db % 4] = cp
-
-    def fdst(p, bb, d):
+            go(rcopy(sc[p].at[dc, db % 4], fdst(p, db, 0), gcs.at[p, db % 4, dc - 1], gcr.at[p, db % 4, dc - 1], C, dc))
+        if db != 2:
+            cp = pltpu.make_async_copy(sc[p].at[0, db % 4], fdst(p, db, 0), gcl.at[p, db % 4])
+            cp.start()
+            locals_[p, db % 4] = cp
+
+    def fdst(p, db, d):
         A, B, C = ORDERS[p]
+        if db == 2:
+            c = wrap(co[C] - d)
+            return lv[p].at[:, c] if A < C else lv[p].at[c, :]
         idx = [None, None, None]
         idx[A] = slice(None)
-        idx[B] = bb
+        idx[B] = wrap(co[B] + db)
         idx[C] = wrap(co[C] - d)
         return F.at[idx[0], idx[1], idx[2], :, pl.ds(gcol[p], GB[p] * 128)]
 
@@ -205,6 +232,7 @@
         for d in (1, 3, 2):
             hbcp[p, d] = go(rcopy(hb[p].at[wrap(co[B] + d)], hc[p].at[d - 1], hbs.at[p, d - 1], hbr.at[p, d - 1], B, d))
     for p in range(3):
+        pltpu.make_async_copy(rc.at[p, pl.ds(0, 15)], rc.at[p, pl.ds(0, 15)], trs.at[p]).wait()
         pack(p, 0)
     for k in range(4):
         for p in range(3):
@@ -254,15 +282,31 @@
         idx[ORDERS[p][1]] = bb
         return ref.at[idx[0], idx[1], idx[2]]
 
-    chunks = [(p, db) for db in (0, -1, 1, 2) for p in range(3)]
+    chunks = [(p, db) for db in (0, -1, 1) for p in range(3)]
+
+    def arrived(p, db):
+        for dc in (1, 3, 2):
+            rcopy(sc[p].at[dc, db % 4], fdst(p, db, dc), gcs.at[p, db % 4, dc - 1], gcr.at[p, db % 4, dc - 1], ORDERS[p][2], dc).wait_recv()
+        if db != 2:
+            locals_[p, db % 4].wait()
+
+    for p in range(3):
+        view = at_b(HV, p, wrap(co[ORDERS[p][1]] + 2))
+        for i in range(4):
+            g2[i * 96:(i + 1) * 96, 0:1024] = view[i].astype(f32).reshape(96, 1024).astype(bf)
+
+        def prod(ct, carry, p=p):
+            cols = pl.ds(pl.multiple_of(ct * 256, 256), 256)
+            wcols = pl.ds(pl.multiple_of(gcol[p] + ct * 256, 256), 256)
+            u = jnp.dot(g2[:, 0:1024], wv[:, wcols], preferred_element_type=f32)
+            U[p][:, :, :, cols] = u.reshape(4, 4, CAP, 256).astype(bf)
+            return carry
+        lax.fori_loop(0, GB[p] // 2, prod, 0)
 
     def load(n):
         p, db = chunks[n]
-        C = ORDERS[p][2]
         bb = wrap(co[ORDERS[p][1]] + db)
-        for dc in (1, 3, 2):
-            rcopy(sc[p].at[dc, db % 4], fdst(p, bb, dc), gcs.at[p, db % 4, dc - 1], gcr.at[p, db % 4, dc - 1], C, dc).wait_recv()
-        locals_[p, db % 4].wait()
+        arrived(p, db)
         gw = GB[p] * 128
         cp = pltpu.make_async_copy(at_b(F, p, bb).at[:, :, :, pl.ds(gcol[p], gw)], gch.at[n % 2, :, :, :, pl.ds(0, gw)], gls.at[n % 2])
         cp.start()
@@ -283,6 +327,12 @@
                                    preferred_element_type=f32)
             q = proj * hview[:, :, :, f * 256:(f + 1) * 256].astype(f32).reshape(384, 256)
             acc = acc + q[:, 0:128] + q[:, 128:256]
+        give(p, db, acc)
+
+    def give(p, db, acc):
+        B = ORDERS[p][1]
+        bb = wrap(co[B] + db)
+        R1, R2 = rest(p)
         pad = jnp.concatenate([acc.reshape(16, CAP, 128), jnp.zeros((16, 8, 128), f32)], axis=1).reshape(512, 128)
         row = jnp.sum(jnp.transpose(pad), axis=0, keepdims=True)
         for i in range(4):
@@ -299,11 +349,25 @@
                                              device_id={"expert": c[0] * 16 + c[1] * 4 + c[2]}, device_id_type=MESH).start()
 
     cur = load(0)
-    for n in range(12):
-        nxt = load(n + 1) if n < 11 else None
+    for n in range(9):
+        nxt = load(n + 1) if n < 8 else None
         cur.wait()
         derive(n)
         cur = nxt
+    lcps = []
+    for p in range(3):
+        arrived(p, 2)
+        cp = pltpu.make_async_copy(lv[p], at_b(F, p, wrap(co[ORDERS[p][1]] + 2)).at[:, :, :, pl.ds(gcol[p], GB[p] * 128)], lvs.at[p])
+        cp.start()
+        lcps.append(cp)
+        quads = []
+        for i in range(4):
+            t = jnp.zeros((4, CAP, 128), f32)
+            for k in range(GB[p]):
+                cols = slice(k * 128, (k + 1) * 128)
+                t = t + U[p][i, :, :, cols].astype(f32) * lv[p][i, :, :, cols].astype(f32)
+            quads.append(t.reshape(96, 128))
+        give(p, 2, jnp.concatenate(quads, axis=0))
 
     home = jnp.zeros((64, 128), f32)
     window = lax.broadcasted_iota(jnp.int32, (64, 128), 1) // 32
@@ -331,12 +395,15 @@
             add = jnp.dot(lt, router[:, gcol[p] + c0:gcol[p] + c0 + 256], preferred_element_type=f32)
             hnd[:, gcol[p] + c0:gcol[p] + c0 + 256] = (gb[p][co[B], co[A], :, c0:c0 + 256].astype(f32) + add).astype(bf)
         cols = pl.ds(gcol[p], gw)
-        cp = pltpu.make_async_remote_copy(src_ref=hnd.at[:, cols], dst_ref=handed.at[:, cols], send_sem=hns.at[p], recv_sem=hnr.at[p],
-                                          device_id=other, device_id_type=MESH)
+        cp = pltpu.make_async_copy(hnd.at[:, cols], handed.at[:, cols], gls.at[p])
         cp.start()
         hcps.append(cp)
     for p in range(3):
         pltpu.make_async_copy(dr.at[p, pl.ds(0, 63)], dr.at[p, pl.ds(0, 63)], dss.at[p]).wait()
+    for p in range(3):
+        pltpu.make_async_copy(rc.at[p, pl.ds(0, 15)], rc.at[p, pl.ds(0, 15)], tss.at[p]).wait()
+    for cp in lcps:
+        cp.wait()
     hout.wait()
     for cp in sends:
         cp.wait_send()
@@ -358,16 +425,17 @@
         in_specs=[vm, vm, vm, any_, any_, any_], out_specs=(any_, any_, any_),
         scratch_shapes=[V((1024, 1024), bf), V((4, 4, 4, CAP, 1024), bf), V((1024, 4096), bf), V((2, 4, 4, CAP, gmax), bf),
                         V((384, gmax), bf), V((3, 4, 4, 1, 128), f32), V((3, 64, 1, 128), f32), V((128, 4096), bf),
-                        V((64, 128), f32), V((64, 128), f32)]
-        + [V((4, 4, 128, g * 128 + 128), bf) for g in GB]
+                        V((64, 128), f32), V((64, 128), f32), V((4, 4, 4, 1, 128), f32), V((3, 16, 4, 1, 128), f32)]
+        + [V((4, 4, CAP, g * 128), bf) for g in GB] * 2
+        + [V((4, 4, 128, g * 128), bf) for g in GB]
         + [V((4, 4, 4, CAP, g * 128), bf) for g in GB]
         + [V((3, 4, 4, CAP, h * 128), bf) for h in HB]
         + [V((4, 4, 4, CAP, h * 128), bf) for h in HB]
         + [V((3, 4, 4, CAP, h * 128), bf) for h in HB]
         + [D((3, 2)), D((3, 4)), D((3, 4)), D((3, 4, 4)), D((3, 4, 4)), D((3, 4, 3)), D((3, 4, 3)), D((3, 4)),
            D((3, 3)), D((3, 3)), D((3, 3)), D((3, 3)), D((3, 4, 3)), D((3, 4, 3)),
-           D((2,)), D((1,)), D((3,)), D((3,)), D((1,)), D((3,)), D((3,))],
-        compiler_params=pltpu.CompilerParams(has_side_effects=True, collective_id=0, vmem_limit_bytes=63 * 2**20),
+           D((3,)), D((1,)), D((3,)), D((3,)), D((1,)), D((3,)), D((3,)), D((3,))],
+        compiler_params=pltpu.CompilerParams(has_side_effects=True, collective_id=0, vmem_limit_bytes=67043328),
     )(routes, scores, router, grad, hidden, down)
     return F.reshape(64 * CAP, 4096), HR.reshape(64 * CAP, 1024), handed
 
@@ -375,7 +443,8 @@
 def body(grad_out, saved_hidden, routes, scores, down_weight, router):
     n_tokens, n_routes, hidden_width = saved_hidden.shape[1:]
     hidden_flat = saved_hidden[0].reshape(n_tokens * n_routes, hidden_width)
-    grad_recv, hidden_recv, handed = exchange(routes[0].T, scores[0].T, router[0], grad_out[0], hidden_flat, down_weight[0, 0])
+    grad_recv, hidden_recv, inp = exchange(routes[0].T, scores[0].T, router[0], grad_out[0], hidden_flat, down_weight[0, 0])
+    handed = lax.ppermute(inp, "section", [(0, 1), (1, 0)])
     weight_out = lax.dot_general(hidden_recv, grad_recv, (((0,), (0,)), ((), ())), preferred_element_type=jnp.float32).astype(jnp.bfloat16)
     return weight_out[None, None], handed[None]
 

time: 199 us -> 195 us (0.980)
  Pallas kernels: 178 us -> 170 us
  starting transfers between devices: 0 us -> 3.61 us
    pallas_call x1, Pallas kernels: 178 us -> 170 us  [exchange(): pl.pallas_call(comm_kernel, out_shape=(jax.ShapeDtypeStruct((4, 4, 4, CAP...]
    ppermute x0 -> x1, starting transfers between devices: none -> 3.61 us  [body(): handed = lax.ppermute(inp, 'section', [(0, 1), (1, 0)])]
  transfers between devices with their start and end apart: 0 -> 1, of which waited for: 0 -> 0; matrix products, arithmetic and copies ran while one was open for 0% -> 10% of each run, Pallas kernels for 0% -> 0%
where the time goes in v5:
time: 195 us
  Pallas kernels  170 us (87%)
  matrix products  19.3 us (10%)
  starting transfers between devices  3.61 us (2%)
    pallas_call x1, Pallas kernels, exchange(): pl.pallas_call(comm_kernel, out_shape=(jax.ShapeDtypeStruct((4, 4, 4, CAP...  170 us
    dot_general x1, matrix products, body(): lax.dot_general(hidden_recv, grad_recv, (((0,), (0,)), ((), ())), preferr...  19.3 us
  transfers between devices with their start and end apart: 1, of which 0 were waited for; matrix products, arithmetic and copies ran while one was open for 10% of the time, Pallas kernels for 0%

profile of v5, /device:TPU:1, one launch (start us, length us, event | category | flops | bytes accessed | tf_op | source)
XLA Modules:
  0.0 194.7 jit_solution(17659397094543513898)
XLA Ops:
  0.6 170.2 %shard_map.77 = (bf16[4,4,4,24,4096]{4,3,2,1,0:T(8,128)(2,1)}, bf16[4,4,4,24,1024]{4,3,2,1,0:T(8,128)(2,1)}, bf16[128,4096]{1,0:T(8,128)(2,1)}) custom-call(s32[8,128]{1,0:T(8,128)} %bitcast.26, f32[8,128]{1,0:T(8,128)} %bitcast.27, bf16[64,4096]{1,0:T(8,128)(2,1)} %bitcast.25, bf16[128,4096]{1,0:T(8,128)(2,1)} %bitcast.23, bf16[1024,1024]{1,0:T(8,128)(2,1)} %bitcast.22, ...), custom_call_target="tpu_custom_call" | custom-call | tf_op jit(solution)/shard_map/pallas_call | solution.py:421
  170.8 3.6 %collective-permute-start = (bf16[128,4096]{1,0:T(8,128)(2,1)}, bf16[128,4096]{1,0:T(8,128)(2,1)S(1)}, u32[]{:S(2)}, u32[]{:S(2)}) collective-permute-start(bf16[128,4096]{1,0:T(8,128)(2,1)} %get-tuple-element.7), channel_id=1, source_target_pairs={{0,64},{64,0},{1,65},{65,1},{2,66},{66,2},{3,67},{67,3},{4,68},{68... | collective-permute-start | bytes 3145736 | tf_op jit(solution)/shard_map/ppermute | solution.py:447
  174.5 19.3 %fusion = bf16[1,1,1024,4096]{3,2,1,0:T(8,128)(2,1)} fusion(bf16[4,4,4,24,1024]{4,3,2,1,0:T(8,128)(2,1)} %get-tuple-element.5, bf16[4,4,4,24,4096]{4,3,2,1,0:T(8,128)(2,1)} %get-tuple-element.6), kind=kOutput, calls=%fused_computation.1 | convolution fusion | flops 12889096192 | bytes 24117248 | tf_op jit(solution)/shard_map/dot_general | solution.py:448
  193.8 0.0 collective-permute-done
  193.8 1.0 copy.10
Async XLA Ops:
  170.8 22.9 %collective-permute-start = (bf16[128,4096]{1,0:T(8,128)(2,1)}, bf16[128,4096]{1,0:T(8,128)(2,1)S(1)}, u32[]{:S(2)}, u32[]{:S(2)}) collective-permute-start(bf16[128,4096]{1,0:T(8,128)(2,1)} %get-tuple-element.7), channel_id=1, source_target_pairs={{0,64},{64,0},{1,65},{65,1},{2,66},{66,2},{3,67},{67,3},{4,68},{68... | collective-permute-start | bytes 3145736 | tf_op jit(solution)/shard_map/ppermute | solution.py:447

commit v6 on v5

--- a/solution.py
+++ b/solution.py
@@ -254,13 +254,13 @@
     for p in range(3):
         hidden_c(p, 0)
     for p in range(3):
-        pack(p, -1)
-    for p in range(3):
-        pack(p, 1)
-    for p in range(3):
         for d in (1, 3, 2):
             hbcp[p, d].wait_recv()
             hidden_c(p, d)
+    for p in range(3):
+        pack(p, -1)
+    for p in range(3):
+        pack(p, 1)
     for p in range(3):
         for k in range(4):
             bcp[p, k][2].wait_recv(); bcp[p, k][3].wait_recv()

time: 195 us -> 184 us (0.944)
  Pallas kernels: 170 us -> 160 us
    pallas_call x1, Pallas kernels: 170 us -> 160 us  [exchange(): pl.pallas_call(comm_kernel, out_shape=(jax.ShapeDtypeStruct((4, 4, 4, CAP...]
  transfers between devices with their start and end apart: 1 -> 1, of which waited for: 0 -> 0; matrix products, arithmetic and copies ran while one was open for 10% -> 11% of each run, Pallas kernels for 0% -> 0%
where the time goes in v6:
time: 184 us
  Pallas kernels  160 us (87%)
  matrix products  19.3 us (10%)
  starting transfers between devices  2.74 us (1%)
    pallas_call x1, Pallas kernels, exchange(): pl.pallas_call(comm_kernel, out_shape=(jax.ShapeDtypeStruct((4, 4, 4, CAP...  160 us
    dot_general x1, matrix products, body(): lax.dot_general(hidden_recv, grad_recv, (((0,), (0,)), ((), ())), preferr...  19.3 us
  transfers between devices with their start and end apart: 1, of which 0 were waited for; matrix products, arithmetic and copies ran while one was open for 11% of the time, Pallas kernels for 0%

profile of v6, /device:TPU:1, one launch (start us, length us, event | category | flops | bytes accessed | tf_op | source)
XLA Modules:
  0.0 183.6 jit_solution(9283284487011932071)
XLA Ops:
  0.6 160.0 %shard_map.77 = (bf16[4,4,4,24,4096]{4,3,2,1,0:T(8,128)(2,1)}, bf16[4,4,4,24,1024]{4,3,2,1,0:T(8,128)(2,1)}, bf16[128,4096]{1,0:T(8,128)(2,1)}) custom-call(s32[8,128]{1,0:T(8,128)} %bitcast.26, f32[8,128]{1,0:T(8,128)} %bitcast.27, bf16[64,4096]{1,0:T(8,128)(2,1)} %bitcast.25, bf16[128,4096]{1,0:T(8,128)(2,1)} %bitcast.23, bf16[1024,1024]{1,0:T(8,128)(2,1)} %bitcast.22, ...), custom_call_target="tpu_custom_call" | custom-call | tf_op jit(solution)/shard_map/pallas_call | solution.py:421
  160.6 2.7 %collective-permute-start = (bf16[128,4096]{1,0:T(8,128)(2,1)}, bf16[128,4096]{1,0:T(8,128)(2,1)S(1)}, u32[]{:S(2)}, u32[]{:S(2)}) collective-permute-start(bf16[128,4096]{1,0:T(8,128)(2,1)} %get-tuple-element.7), channel_id=1, source_target_pairs={{0,64},{64,0},{1,65},{65,1},{2,66},{66,2},{3,67},{67,3},{4,68},{68... | collective-permute-start | bytes 3145736 | tf_op jit(solution)/shard_map/ppermute | solution.py:447
  163.4 19.3 %fusion = bf16[1,1,1024,4096]{3,2,1,0:T(8,128)(2,1)} fusion(bf16[4,4,4,24,1024]{4,3,2,1,0:T(8,128)(2,1)} %get-tuple-element.5, bf16[4,4,4,24,4096]{4,3,2,1,0:T(8,128)(2,1)} %get-tuple-element.6), kind=kOutput, calls=%fused_computation.1 | convolution fusion | flops 12889096192 | bytes 24117248 | tf_op jit(solution)/shard_map/dot_general | solution.py:448
  182.7 0.0 collective-permute-done
  182.7 1.0 copy.10
Async XLA Ops:
  160.6 22.0 %collective-permute-start = (bf16[128,4096]{1,0:T(8,128)(2,1)}, bf16[128,4096]{1,0:T(8,128)(2,1)S(1)}, u32[]{:S(2)}, u32[]{:S(2)}) collective-permute-start(bf16[128,4096]{1,0:T(8,128)(2,1)} %get-tuple-element.7), channel_id=1, source_target_pairs={{0,64},{64,0},{1,65},{65,1},{2,66},{66,2},{3,67},{67,3},{4,68},{68... | collective-permute-start | bytes 3145736 | tf_op jit(solution)/shard_map/ppermute | solution.py:447

commit v7 on v6

--- a/solution.py
+++ b/solution.py
@@ -49,10 +49,6 @@
     for axis in range(3):
         for d in (1, 2, 3):
             pl.semaphore_signal(barrier, inc=1, device_id=peer(axis, d), device_id_type=MESH)
-    for p in range(3):
-        for da in (1, 2, 3):
-            for db in (1, 2, 3):
-                pl.semaphore_signal(barrier, inc=1, device_id=plane(p, da, db)[1], device_id_type=MESH)
 
     sends = []
 
@@ -88,7 +84,7 @@
         acp.append(ring(p, A, lambda d, p=p, A=A, B=B: gb[p].at[co[B], wrap(co[A] + d)], gas, gar, (p,)))
         for k, da in enumerate((0, -1, 1, 2)):
             bcp[p, k] = ring(p, B, lambda d, p=p, A=A, B=B, da=da: gb[p].at[wrap(co[B] + d), wrap(co[A] + da)], gbs, gbr, (p, k))
-    pl.semaphore_wait(barrier, 36)
+    pl.semaphore_wait(barrier, 9)
     for p in range(3):
         loads[p].wait()
         go(acp[p][0]); go(acp[p][1])
@@ -115,20 +111,6 @@
     for k in range(64):
         tab[k // 16, (k // 4) % 4, k % 4] = code_e[k:k + 1, :]
 
-    for p, (A, B, C) in enumerate(ORDERS):
-        for da in range(4):
-            for db in range(4):
-                c, dev = plane(p, da, db)
-                idx = list(c)
-                if da == 0 and db == 0:
-                    for k in range(4):
-                        idx[C] = k
-                        rc[p, co[B] * 4 + co[A], k] = tab[idx[0], idx[1], idx[2]]
-                    continue
-                idx[C] = slice(None)
-                pltpu.make_async_remote_copy(src_ref=tab.at[idx[0], idx[1], idx[2]], dst_ref=rc.at[p, co[B] * 4 + co[A]],
-                                             send_sem=tss.at[p], recv_sem=trs.at[p], device_id=dev, device_id_type=MESH).start()
-
     slots = jnp.concatenate([jnp.sum(jnp.where(eio == ri[k:k + 1, :], rank, 0.0), axis=0, keepdims=True) for k in range(8)], axis=0)
     n8 = lax.broadcasted_iota(jnp.int32, (128, 1024), 1) // 8
     spread = jnp.where(n8 == lax.broadcasted_iota(jnp.int32, (128, 1024), 0), 1.0, 0.0).astype(bf)
@@ -173,6 +155,20 @@
     for p in range(3):
         acp[p][2].wait_recv(); acp[p][3].wait_recv()
         go(bcp[p, 3][0]); go(bcp[p, 3][1])
+
+    for p, (A, B, C) in enumerate(ORDERS):
+        for da in range(4):
+            for db in range(4):
+                c, dev = plane(p, da, db)
+                idx = list(c)
+                if da == 0 and db == 0:
+                    for k in range(4):
+                        idx[C] = k
+                        rc[p, co[B] * 4 + co[A], k] = tab[idx[0], idx[1], idx[2]]
+                    continue
+                idx[C] = slice(None)
+                pltpu.make_async_remote_copy(src_ref=tab.at[idx[0], idx[1], idx[2]], dst_ref=rc.at[p, co[B] * 4 + co[A]],
+                                             send_sem=tss.at[p], recv_sem=trs.at[p], device_id=dev, device_id_type=MESH).start()
 
     j = lax.broadcasted_iota(jnp.int32, (4 * CAP, 1), 0)
     dCj = (j >= CAP).astype(jnp.int32) + (j >= 2 * CAP).astype(jnp.int32) + (j >= 3 * CAP).astype(jnp.int32)
@@ -391,9 +387,9 @@
     hcps = []
     for p, (A, B, C) in enumerate(ORDERS):
         gw = GB[p] * 128
-        for c0 in range(0, gw, 256):
-            add = jnp.dot(lt, router[:, gcol[p] + c0:gcol[p] + c0 + 256], preferred_element_type=f32)
-            hnd[:, gcol[p] + c0:gcol[p] + c0 + 256] = (gb[p][co[B], co[A], :, c0:c0 + 256].astype(f32) + add).astype(bf)
+        for c0 in range(0, gw, gw // 2):
+            add = jnp.dot(lt, router[:, gcol[p] + c0:gcol[p] + c0 + gw // 2], preferred_element_type=f32)
+            hnd[:, gcol[p] + c0:gcol[p] + c0 + gw // 2] = (gb[p][co[B], co[A], :, c0:c0 + gw // 2].astype(f32) + add).astype(bf)
         cols = pl.ds(gcol[p], gw)
         cp = pltpu.make_async_copy(hnd.at[:, cols], handed.at[:, cols], gls.at[p])
         cp.start()

time: 184 us -> 183 us (level)
  no operation moved by 1% of the time
where the time goes in v7:
time: 183 us
  Pallas kernels  159 us (87%)
  matrix products  19.3 us (11%)
  starting transfers between devices  2.65 us (1%)
    pallas_call x1, Pallas kernels, exchange(): pl.pallas_call(comm_kernel, out_shape=(jax.ShapeDtypeStruct((4, 4, 4, CAP...  159 us
    dot_general x1, matrix products, body(): lax.dot_general(hidden_recv, grad_recv, (((0,), (0,)), ((), ())), preferr...  19.3 us
  transfers between devices with their start and end apart: 1, of which 0 were waited for; matrix products, arithmetic and copies ran while one was open for 11% of the time, Pallas kernels for 0%

profile of v7, /device:TPU:1, one launch (start us, length us, event | category | flops | bytes accessed | tf_op | source)
XLA Modules:
  0.0 182.7 jit_solution(15955159369097169649)
XLA Ops:
  0.6 159.1 %shard_map.77 = (bf16[4,4,4,24,4096]{4,3,2,1,0:T(8,128)(2,1)}, bf16[4,4,4,24,1024]{4,3,2,1,0:T(8,128)(2,1)}, bf16[128,4096]{1,0:T(8,128)(2,1)}) custom-call(s32[8,128]{1,0:T(8,128)} %bitcast.26, f32[8,128]{1,0:T(8,128)} %bitcast.27, bf16[64,4096]{1,0:T(8,128)(2,1)} %bitcast.25, bf16[128,4096]{1,0:T(8,128)(2,1)} %bitcast.23, bf16[1024,1024]{1,0:T(8,128)(2,1)} %bitcast.22, ...), custom_call_target="tpu_custom_call" | custom-call | tf_op jit(solution)/shard_map/pallas_call | solution.py:417
  159.8 2.7 %collective-permute-start = (bf16[128,4096]{1,0:T(8,128)(2,1)}, bf16[128,4096]{1,0:T(8,128)(2,1)S(1)}, u32[]{:S(2)}, u32[]{:S(2)}) collective-permute-start(bf16[128,4096]{1,0:T(8,128)(2,1)} %get-tuple-element.7), channel_id=1, source_target_pairs={{0,64},{64,0},{1,65},{65,1},{2,66},{66,2},{3,67},{67,3},{4,68},{68... | collective-permute-start | bytes 3145736 | tf_op jit(solution)/shard_map/ppermute | solution.py:443
  162.4 19.3 %fusion = bf16[1,1,1024,4096]{3,2,1,0:T(8,128)(2,1)} fusion(bf16[4,4,4,24,1024]{4,3,2,1,0:T(8,128)(2,1)} %get-tuple-element.5, bf16[4,4,4,24,4096]{4,3,2,1,0:T(8,128)(2,1)} %get-tuple-element.6), kind=kOutput, calls=%fused_computation.1 | convolution fusion | flops 12889096192 | bytes 24117248 | tf_op jit(solution)/shard_map/dot_general | solution.py:444
  181.7 0.0 collective-permute-done
  181.7 1.0 copy.10
Async XLA Ops:
  159.8 22.0 %collective-permute-start = (bf16[128,4096]{1,0:T(8,128)(2,1)}, bf16[128,4096]{1,0:T(8,128)(2,1)S(1)}, u32[]{:S(2)}, u32[]{:S(2)}) collective-permute-start(bf16[128,4096]{1,0:T(8,128)(2,1)} %get-tuple-element.7), channel_id=1, source_target_pairs={{0,64},{64,0},{1,65},{65,1},{2,66},{66,2},{3,67},{67,3},{4,68},{68... | collective-permute-start | bytes 3145736 | tf_op jit(solution)/shard_map/ppermute | solution.py:443
